TPU v7x, 32 devices: a whole 2x2x4 slice. The times are simulated.
32 devices in a mesh: rep: 4 (over z), row: 4 (over x, core), col: 2 (over y).
Axes of the slice: x: 2, y: 2, z: 4, core: 2. Of those that a mesh axis runs over, the one named last changes fastest.
Arguments:
- grad_parts: bfloat16 [4, 16384, 6144], P('rep', ('row', 'col')), may hold values from -0.03125 to 0.03125, as said below
- statistic: float32 [6144, 6144], P('row', 'col'), may hold values from -150 to 150, as said below
Outputs:
- gram_matrix: float32 [6144, 6144], P('row', 'col')
- statistic_next: float32 [6144, 6144], P('row', 'col')
Inputs may be any that keep to these rules, and one draw needn't show every extreme that they name: Every entry of grad_parts has a magnitude between 2^-10 and 2^-5. statistic is symmetric and positive definite.
All inputs are finite; a program needn't handle non-finite values.
Results may differ from a plain program's by a relative error of at most 0.008.
Values may be sent and summed in bfloat16 or wider, within the bound.
No kernel may reach another device: no remote copies, remote signals or barrier semaphores. Data moves between devices by JAX's collectives and lax.ppermute only.
A program may use at most 192 MiB of HBM per device.

v0:
```python
import jax
import jax.numpy as jnp
from jax import lax
from jax.sharding import PartitionSpec as P


def shards(grad_parts, statistic):
    own_part = grad_parts[0].astype(jnp.float32)
    summed = lax.psum_scatter(own_part.astype(jnp.bfloat16), "rep", scatter_dimension=0, tiled=True)
    rows_panel = lax.all_to_all(summed, "row", split_axis=1, concat_axis=0, tiled=True)
    cols_panel = lax.all_to_all(summed, "col", split_axis=1, concat_axis=0, tiled=True)
    row_count = lax.axis_size("row")
    col_count = lax.axis_size("col")
    quarter = summed.shape[0]
    left_whole = lax.all_gather(rows_panel, "col", axis=0, tiled=True)
    left_order = (
        left_whole.reshape(col_count, row_count, quarter, -1)
        .transpose(1, 0, 2, 3)
        .reshape(row_count * col_count * quarter, -1)
    )
    partial_tile = lax.dot_general(
        left_order,
        lax.all_gather(cols_panel, "row", axis=0, tiled=True),
        (((0,), (0,)), ((), ())),
        preferred_element_type=jnp.float32,
    )
    gram_tile = lax.psum(partial_tile, "rep")
    return (gram_tile, 0.95 * statistic + 0.05 * gram_tile)


def solution(mesh):
    return jax.shard_map(
        shards,
        mesh=mesh,
        in_specs=(P("rep", ("row", "col"), None), P("row", "col")),
        out_specs=(P("row", "col"), P("row", "col")),
        check_vma=False,
    )
```

profile of v0, /device:TPU:0, one launch (start us, length us, event | category | flops | bytes accessed | tf_op | source)
XLA Modules:
  0.0 1626.5 jit_solution(12246390620208611394)
XLA Ops:
  7.2 0.0 reduce-scatter.2.cloned.1.call-start
  7.2 30.3 %copy.5 = bf16[1,2048,6144]{1,2,0:T(8,128)(2,1)} copy(bf16[1,2048,6144]{2,1,0:T(8,128)(2,1)} %param.2) | data formatting | bytes 50331648 | tf_op args[0]
  37.5 0.0 reduce-scatter.2.cloned.1.call-update
  37.6 0.0 all-gather.3.cloned.1.call-start
  37.6 417.0 %reduce-scatter.2.cloned.1.call-done = bf16[512,6144]{0,1:T(8,128)(2,1)} async-done(((bf16[2048,6144]{0,1:T(8,128)(2,1)}), bf16[512,6144]{0,1:T(8,128)(2,1)}) %reduce-scatter.2.cloned.1.call-update) | async-done | bytes 6291472 | tf_op jit(solution)/shard_map/reduce_scatter | solution.py:9
  454.7 77.3 %all_to_all.38 = bf16[512,4,1536]{0,2,1:T(8,128)(2,1)} all-to-all(bf16[512,4,1536]{0,2,1:T(8,128)(2,1)} %bitcast.15), channel_id=1, replica_groups=mesh['rep'=4,'row'=4,'col'=2] {'row'}, dimensions={1} | all-to-all | bytes 12582912 | tf_op jit(solution)/shard_map/all_to_all | solution.py:10
  532.0 8.6 copy.6
  540.6 0.0 all-gather.3.cloned.1.call-update
  540.6 0.0 all-gather.5.cloned.1.call-start
  540.7 140.8 %all_to_all.39 = bf16[512,2,3072]{0,2,1:T(8,128)(2,1)} all-to-all(bf16[512,2,3072]{0,2,1:T(8,128)(2,1)} %bitcast.16), channel_id=1, replica_groups=mesh['rep'=4,'row'=4,'col'=2] {'col'}, dimensions={1} | all-to-all | bytes 12582912 | tf_op jit(solution)/shard_map/all_to_all | solution.py:11
  681.4 8.6 copy.8
  690.1 0.0 all-gather.5.cloned.1.call-update
  690.1 0.0 all-reduce.2.cloned.1.call-start
  690.2 64.5 %all-gather.3.cloned.1.call-done = bf16[4096,1536]{1,0:T(8,128)(2,1)} async-done(((bf16[2048,1536]{1,0:T(8,128)(2,1)}), bf16[4096,1536]{1,0:T(8,128)(2,1)}) %all-gather.3.cloned.1.call-update) | async-done | bytes 12582928 | tf_op jit(solution)/shard_map/all_gather | solution.py:15
  754.7 11.1 copy.7
  765.8 145.7 %all-gather.5.cloned.1.call-done = bf16[4096,3072]{1,0:T(8,128)(2,1)} async-done(((bf16[1024,3072]{1,0:T(8,128)(2,1)}), bf16[4096,3072]{1,0:T(8,128)(2,1)}) %all-gather.5.cloned.1.call-update) | async-done | bytes 25165840 | tf_op jit(solution)/shard_map/all_gather | solution.py:23
  911.5 48.0 %fusion = f32[1536,3072]{1,0:T(8,128)} fusion(bf16[4096,1536]{1,0:T(8,128)(2,1)} %bitcast.21, bf16[4096,3072]{1,0:T(8,128)(2,1)} %all-gather.5.cloned.1.call-done), kind=kOutput, calls=%fused_computation.1 | convolution fusion | flops 38654705664 | bytes 56623104 | tf_op jit(solution)/shard_map/dot_general | solution.py:21
  959.5 0.0 all-reduce.2.cloned.1.call-update
  959.6 629.5 %all-reduce.2.cloned.1.call-done = f32[1536,3072]{1,0:T(8,128)} async-done(((f32[1536,3072]{1,0:T(8,128)}), f32[1536,3072]{1,0:T(8,128)}) %all-reduce.2.cloned.1.call-update) | async-done | bytes 18874384 | tf_op jit(solution)/shard_map/psum | solution.py:27
  1589.1 0.0 copy-start
  1589.1 20.7 %multiply_add_fusion = f32[1536,3072]{1,0:T(8,128)} fusion(f32[1536,3072]{1,0:T(8,128)} %all-reduce.2.cloned.1.call-done, f32[1536,3072]{1,0:T(8,128)} %param.3), kind=kLoop, calls=%fused_computation | loop fusion | flops 14155776 | bytes 56623104 | tf_op jit(solution)/shard_map/add | solution.py:28
  1609.8 3.3 copy-done
  1613.1 6.8 copy.10
Async XLA Ops:
  7.2 447.5 %reduce-scatter.2.cloned.1.call-start = ((), (), s32[]{:S(2)}) async-start(), calls=%async_computation.3 | async-start | bytes 31457280 | tf_op jit(solution)/shard_map/reduce_scatter | solution.py:9
  37.6 717.1 %all-gather.3.cloned.1.call-start = ((), (), s32[]{:S(2)}) async-start(), calls=%async_computation.4 | async-start | bytes 18874368 | tf_op jit(solution)/shard_map/all_gather | solution.py:15
  540.6 370.9 %all-gather.5.cloned.1.call-start = ((), (), s32[]{:S(2)}) async-start(), calls=%async_computation.5 | async-start | bytes 31457280 | tf_op jit(solution)/shard_map/all_gather | solution.py:23
  690.1 899.0 %all-reduce.2.cloned.1.call-start = ((), (), s32[]{:S(2)}) async-start(), calls=%async_computation.6 | async-start | bytes 37748736 | tf_op jit(solution)/shard_map/psum | solution.py:27
  1589.1 24.0 %copy-start = (f32[1536,3072]{1,0:T(8,128)S(1)}, f32[1536,3072]{1,0:T(8,128)}, u32[]{:S(2)}) copy-start(f32[1536,3072]{1,0:T(8,128)} %all-reduce.2.cloned.1.call-done) | copy-start | bytes 56623108
Sparse Core Ops, SparseCore 0:
  37.7 416.9 reduce-scatter.1
  540.7 213.8 all-gather.2
  756.2 155.2 all-gather.4
  959.7 629.3 all-reduce.1
where the time goes:
time: 1630 us
  waiting for transfers between devices  1260 us (77%)
  blocking collectives  218 us (13%)
  local copies, waits for them, and re-layouts  68.9 us (4%)
  matrix products  48 us (3%)
  other arithmetic  20.7 us (1%)
    psum x1, waiting for transfers between devices, shards(): gram_tile = lax.psum(partial_tile, 'rep')  630 us
    reduce_scatter x1, waiting for transfers between devices, shards(): lax.psum_scatter(own_part.astype(jnp.bfloat16), 'rep', scatter_dimension=...  417 us
    all_gather x1, waiting for transfers between devices, shards(): lax.all_gather(cols_panel, 'row', axis=0, tiled=True)  146 us
    all_to_all x1, blocking collectives, shards(): lax.all_to_all(summed, 'col', split_axis=1, concat_axis=0, tiled=True)  141 us
    all_to_all x1, blocking collectives, shards(): lax.all_to_all(summed, 'row', split_axis=1, concat_axis=0, tiled=True)  77.3 us
    all_gather x1, waiting for transfers between devices, shards(): left_whole = lax.all_gather(rows_panel, 'col', axis=0, tiled=True)  64.5 us
    dot_general x1, matrix products, shards(): lax.dot_general(left_order, lax.all_gather(cols_panel, 'row', axis=0, til...  48 us
    unnamed x4, local copies, waits for them, and re-layouts  40.5 us
  transfers between devices with their start and end apart: 4, of which 4 were waited for; matrix products, arithmetic and copies ran while one was open for 1% of the time, Pallas kernels for 0%

commit v1 on v0

v1 whole, which is shorter than its diff:
```python
import jax
import jax.numpy as jnp
from jax import lax
from jax.experimental import pallas as pl
from jax.experimental.pallas import tpu as pltpu
from jax.sharding import PartitionSpec as P


STRIPS = 6
PER = 1
LAG = 2
GROUPS = (
    ((0, 0), (1, 0), (1, 1)),
    *(tuple((j, i) for i in range(j + 1)) for j in range(2, STRIPS - 1)),
    tuple((STRIPS - 1, i) for i in range(STRIPS // 2)),
    tuple((STRIPS - 1, i) for i in range(STRIPS // 2, STRIPS)),
)
F32 = jnp.float32
BF16 = jnp.bfloat16


def generic(grad_parts, statistic):
    own_part = grad_parts[0].astype(F32)
    summed = lax.psum_scatter(own_part.astype(BF16), "rep", scatter_dimension=0, tiled=True)
    rows_panel = lax.all_to_all(summed, "row", split_axis=1, concat_axis=0, tiled=True)
    cols_panel = lax.all_to_all(summed, "col", split_axis=1, concat_axis=0, tiled=True)
    row_count = lax.axis_size("row")
    col_count = lax.axis_size("col")
    quarter = summed.shape[0]
    left_whole = lax.all_gather(rows_panel, "col", axis=0, tiled=True)
    left_order = (
        left_whole.reshape(col_count, row_count, quarter, -1)
        .transpose(1, 0, 2, 3)
        .reshape(row_count * col_count * quarter, -1)
    )
    partial_tile = lax.dot_general(
        left_order,
        lax.all_gather(cols_panel, "row", axis=0, tiled=True),
        (((0,), (0,)), ((), ())),
        preferred_element_type=F32,
    )
    gram_tile = lax.psum(partial_tile, "rep")
    return (gram_tile, 0.95 * statistic + 0.05 * gram_tile)


def hop_add(idx, t, own, recv, strip, slot, chunk, want_send):
    rows = own.shape[0]
    cuts = 2
    block = rows // cuts
    has_recv = recv is not None
    has_strip = strip is not None
    want_sum = slot is not None

    def body(idx_ref, *refs):
        refs = list(refs)
        value = refs.pop(0)[...]
        if has_recv:
            value = (value.astype(F32) + refs.pop(0)[...].astype(F32)).astype(BF16)
        if has_strip:
            refs.pop(0)
        if want_send:
            refs.pop(0)[...] = value
        if want_sum:
            refs.pop(0)[...] = value

    flat = pl.BlockSpec((block, chunk), lambda i, idx: (i, 0))
    own_spec = pl.BlockSpec((block, chunk), lambda i, idx: (i, idx[t]))
    in_specs = [own_spec]
    operands = [own]
    if has_recv:
        in_specs.append(flat)
        operands.append(recv)
    alias = {}
    if has_strip:
        alias = {1 + len(operands): int(want_send)}
        in_specs.append(pl.BlockSpec(memory_space=pl.ANY))
        operands.append(strip)
    out_specs, out_shape = [], []
    if want_send:
        out_specs.append(flat)
        out_shape.append(jax.ShapeDtypeStruct((rows, chunk), BF16))
    if want_sum:
        out_specs.append(pl.BlockSpec((block, chunk), lambda i, idx: (i, slot)))
        out_shape.append(jax.ShapeDtypeStruct((rows, 2 * PER * chunk), BF16))
    outs = pl.pallas_call(
        body,
        grid_spec=pltpu.PrefetchScalarGridSpec(
            num_scalar_prefetch=1, grid=(cuts,), in_specs=in_specs, out_specs=out_specs
        ),
        out_shape=out_shape,
        input_output_aliases=alias,
        compiler_params=pltpu.CompilerParams(vmem_limit_bytes=46 * 1024 * 1024),
        cost_estimate=pl.CostEstimate(flops=rows * chunk, bytes_accessed=8 * rows * chunk, transcendentals=0),
        name="hop_add",
    )(idx, *operands)
    outs = list(outs)
    return (outs.pop(0) if want_send else None), (outs.pop(0) if want_sum else strip)


def multiply(tab, strips, pairs, width):
    half = width // 2
    depth = strips[0].shape[0]
    lefts = sorted({j for j, _ in pairs})
    rights = sorted({i for _, i in pairs})
    steps = 2 * len(pairs)
    first = {j: 2 * min(p for p, pair in enumerate(pairs) if pair[0] == j) for j in lefts}

    def body(tab_ref, *refs):
        left_refs = {j: (refs[2 * k], refs[2 * k + 1]) for k, j in enumerate(lefts)}
        base = 2 * len(lefts)
        right_refs = {i: (refs[base + 2 * k], refs[base + 2 * k + 1]) for k, i in enumerate(rights)}
        send, keep, turned = refs[-3:]
        n = pl.program_id(0)
        core = tab_ref[2]
        for j in lefts:

            @pl.when(n == first[j])
            def _(j=j):
                for d in range(2):
                    turned[d * half : (d + 1) * half, :] = left_refs[j][d][...].T

        for i in rights:
            mine = [p for p, pair in enumerate(pairs) if pair[1] == i]

            @pl.when((n >= 2 * mine[0]) & (n < 2 * mine[-1] + 2))
            def _(i=i):
                far = jnp.dot(turned[...], right_refs[i][0][...], preferred_element_type=F32)
                near = jnp.dot(turned[...], right_refs[i][1][...], preferred_element_type=F32)
                send[0, :, :] = far[:half].astype(BF16)
                keep[1, :, :] = near[half:]

                @pl.when(core == 0)
                def _():
                    send[1, :, :] = near[:half].astype(BF16)
                    keep[0, :, :] = far[half:]

                @pl.when(core != 0)
                def _():
                    send[1, :, :] = far[half:].astype(BF16)
                    keep[0, :, :] = near[:half]

    in_specs, operands = [], []
    for j in lefts:
        for d in range(2):
            in_specs.append(pl.BlockSpec((depth, half), lambda n, tab, d=d: (0, tab[d])))
            operands.append(strips[j])
    for i in rights:
        mine = [p for p, pair in enumerate(pairs) if pair[1] == i]
        lo, hi = 2 * mine[0], 2 * mine[-1] + 2
        for d in range(2):
            in_specs.append(
                pl.BlockSpec(
                    (depth, half),
                    lambda n, tab, d=d, lo=lo, hi=hi: (
                        0,
                        2 * d + jnp.where(n < lo, 0, jnp.where(n >= hi, 1, n % 2)),
                    ),
                )
            )
            operands.append(strips[i])
    cols = steps * half
    out = pl.BlockSpec((2, half, half), lambda n, tab: (0, 0, n))
    return pl.pallas_call(
        body,
        grid_spec=pltpu.PrefetchScalarGridSpec(
            num_scalar_prefetch=1,
            grid=(steps,),
            in_specs=in_specs,
            out_specs=[out, out],
            scratch_shapes=[pltpu.VMEM((width, depth), BF16)],
        ),
        out_shape=[
            jax.ShapeDtypeStruct((2, half, cols), BF16),
            jax.ShapeDtypeStruct((2, half, cols), F32),
        ],
        compiler_params=pltpu.CompilerParams(vmem_limit_bytes=46 * 1024 * 1024),
        cost_estimate=pl.CostEstimate(
            flops=4 * width * depth * cols, bytes_accessed=4 * depth * cols, transcendentals=0
        ),
        name="multiply",
    )(tab, *operands)


def assemble(place, own_me, own_other, mir_me, mir_other, statistic, width):
    half = width // 2
    rows, cols = statistic.shape
    here = rows // width
    n_groups = len(GROUPS)

    def own_at(g, j, i):
        start, first = GROUPS[g][0]
        final = GROUPS[g][-1][1]
        if g == 0:
            return (j <= 1) & (i <= j), jnp.where(j == 0, 0, 1 + jnp.minimum(i, 1))
        return (j == start) & (i >= first) & (i <= final), jnp.clip(i - first, 0, final - first)

    def body(place_ref, *refs):
        me = refs[:n_groups]
        other = refs[n_groups : 2 * n_groups]
        m_me = refs[2 * n_groups : 3 * n_groups]
        m_other = refs[3 * n_groups : 4 * n_groups]
        stat, gram_out, stat_out = refs[4 * n_groups :]
        core = place_ref[0]
        j = core * here + pl.program_id(0)
        i = pl.program_id(1)
        for g in range(n_groups):
            lower, _ = own_at(g, j, i)
            upper, _ = own_at(g, i, j)

            @pl.when(lower & (core == 0))
            def _(g=g):
                gram_out[:half, :] = me[g][...]
                gram_out[half:, :] = other[g][...].astype(F32)

            @pl.when(lower & (core != 0))
            def _(g=g):
                gram_out[:half, :] = other[g][...].astype(F32)
                gram_out[half:, :] = me[g][...]

            @pl.when(upper & (i > j) & (core == 0))
            def _(g=g):
                gram_out[:, :half] = m_me[g][...].astype(F32).T
                gram_out[:, half:] = m_other[g][...].astype(F32).T

            @pl.when(upper & (i > j) & (core != 0))
            def _(g=g):
                gram_out[:, :half] = m_other[g][...].astype(F32).T
                gram_out[:, half:] = m_me[g][...].astype(F32).T

        stat_out[...] = 0.95 * stat[...] + 0.05 * gram_out[...]

    def low(g):
        def index(r, c, place):
            on, at = own_at(g, place[0] * here + r, c)
            return (0, jnp.where(on, at, 0))

        return pl.BlockSpec((half, width), index)

    def up(g):
        def index(r, c, place):
            j = place[0] * here + r
            on, at = own_at(g, c, j)
            return (0, jnp.where(on & (c > j), at, 0))

        return pl.BlockSpec((half, width), index)

    tile = pl.BlockSpec((width, width), lambda r, c, place: (r, c))
    every = range(n_groups)
    return pl.pallas_call(
        body,
        grid_spec=pltpu.PrefetchScalarGridSpec(
            num_scalar_prefetch=1,
            grid=(here, cols // width),
            in_specs=2 * [low(g) for g in every] + 2 * [up(g) for g in every] + [tile],
            out_specs=[tile, tile],
        ),
        out_shape=[jax.ShapeDtypeStruct((rows, cols), F32)] * 2,
        compiler_params=pltpu.CompilerParams(vmem_limit_bytes=28 * 1024 * 1024),
        name="assemble",
    )(place, *own_me, *own_other, *mir_me, *mir_other, statistic)


def shards(grad_parts, statistic):
    return update(grad_parts, statistic)


def update(grad_parts, statistic):
    own = grad_parts[0]
    reps = lax.axis_size("rep")
    rows_n = lax.axis_size("row")
    z = lax.axis_index("rep")
    r = lax.axis_index("row")
    x = r // 2
    core = r % 2
    y = lax.axis_index("col")
    panel = own.shape[1] // 2
    chunk = panel // (STRIPS * PER)
    width = chunk * PER
    n_chunks = STRIPS * PER * 2
    last = reps - 1
    steps = n_chunks + LAG * last
    end = (z == 0) | (z == last)

    depth = jnp.where(core == 0, z, last - z)
    c = jnp.clip(jnp.arange(steps) - LAG * depth, 0, n_chunks - 1)
    side = jnp.where((c // PER) % 2 == 0, 1 - y, y)
    idx = (side * (STRIPS * PER) + (c // (2 * PER)) * PER + c % PER).astype(jnp.int32)
    tab = jnp.stack([2 * (x != y) + core, 2 * (x == y) + core, core]).astype(jnp.int32)

    swap_core = [(i, i ^ 1) for i in range(rows_n)]

    def grid_pairs(move):
        pairs = []
        for a in range(2):
            for k in range(2):
                for b in range(2):
                    a2, k2, b2 = move(a, k, b)
                    pairs.append(((2 * a + k) * 2 + b, (2 * a2 + k2) * 2 + b2))
        return pairs

    phase_1 = grid_pairs(lambda a, k, b: (a, k, 1 - b) if k else (1 - a, k, b))
    phase_2 = grid_pairs(lambda a, k, b: (1 - a, k, b) if k else (a, k, 1 - b))
    mirror = grid_pairs(lambda a, k, b: (b, k, a))
    rc = ("row", "col")

    recvs = {}
    strips_own = []
    strip = None
    for s in range(steps):
        want_send = s < n_chunks + LAG * (last - 1)
        q = s - LAG * last
        slot = q % (2 * PER) if q >= 0 else None
        if slot == 0:
            strip = None
        send, strip = hop_add(idx, s, own, recvs.get(s - LAG), strip, slot, chunk, want_send)
        if want_send:
            pairs = []
            for k in range(last):
                if 0 <= s - LAG * k < n_chunks:
                    for i in range(rows_n):
                        a, b = (k, k + 1) if i % 2 == 0 else (last - k, last - k - 1)
                        pairs.append((a * rows_n + i, b * rows_n + i))
            recvs[s] = lax.ppermute(send, ("rep", "row"), pairs)
        if slot == 2 * PER - 1:
            strips_own.append(strip)

    holder = z == jnp.where(core == 0, last, 0)
    strips = []
    own_me, own_other, mir_me, mir_other = [], [], [], []
    for pairs in GROUPS:
        while len(strips) <= pairs[-1][0]:
            mine = strips_own[len(strips)]
            other = lax.ppermute(mine, "row", swap_core)
            strips.append(jnp.where(holder, mine, other))
        away, keep = multiply(tab, strips, pairs, width)
        got = lax.ppermute(away, rc, phase_1)
        mid = (keep[0] + got[0].astype(F32)).astype(BF16)
        got_2 = lax.ppermute(mid, rc, phase_2)
        part = (keep[1] + got[1].astype(F32) + got_2.astype(F32)).astype(BF16)

        cur = part
        total = jnp.where(end, part.astype(F32), 0.0)
        for k in range(last):
            cur = lax.ppermute(cur, "rep", sorted({(k, k + 1), (last - k, last - k - 1)}))
            total = total + cur.astype(F32)
        low = total.astype(BF16)
        there = lax.ppermute(low, rc, mirror)
        owner = pairs[-1][0] // (STRIPS // 2)
        own_other.append(lax.ppermute(low, "row", [(i, i ^ 1) for i in range(rows_n) if i % 2 != owner]))
        mir_other.append(lax.ppermute(there, "row", swap_core))
        own_me.append(total)
        mir_me.append(there)

    place = core[None].astype(jnp.int32)
    return tuple(assemble(place, own_me, own_other, mir_me, mir_other, statistic, width))


def solution(mesh):
    sizes = mesh.shape
    paired = sizes["row"] == 4 and sizes["col"] == 2 and sizes["rep"] == 4
    return jax.shard_map(
        shards if paired else generic,
        mesh=mesh,
        in_specs=(P("rep", ("row", "col"), None), P("row", "col")),
        out_specs=(P("row", "col"), P("row", "col")),
        check_vma=False,
    )
```

time: 1630 us -> 802 us (0.49)
  the two profiles are of different devices: /device:TPU:0 before, /device:TPU:3 now
where the time goes in v1:
time: 802 us; the launch traced here: 791 us
  waiting for transfers between devices  299 us (37%)
  starting transfers between devices  260 us (32%)
  Pallas kernels  179 us (22%)
  other arithmetic  49 us (6%)
    ppermute x16, waiting for transfers between devices, update(): recvs[s] = lax.ppermute(send, ('rep', 'row'), pairs)  130 us
    ppermute x6, starting transfers between devices, update(): other = lax.ppermute(mine, 'row', swap_core)  130 us
    pallas_call x6, Pallas kernels, multiply(): pl.pallas_call(body, grid_spec=pltpu.PrefetchScalarGridSpec(num_scalar_pr...  97 us
    ppermute x18, waiting for transfers between devices, update(): lax.ppermute(cur, 'rep', sorted({(k, k + 1), (last - k, last - k - 1)}))  63.7 us
    pallas_call x18, Pallas kernels, hop_add(): pl.pallas_call(body, grid_spec=pltpu.PrefetchScalarGridSpec(num_scalar_pr...  57.6 us
    ppermute x6, waiting for transfers between devices, update(): there = lax.ppermute(low, rc, mirror)  55.8 us
    ppermute x18, starting transfers between devices, update(): lax.ppermute(cur, 'rep', sorted({(k, k + 1), (last - k, last - k - 1)}))  46.3 us
    ppermute x6, waiting for transfers between devices, update(): got = lax.ppermute(away, rc, phase_1)  38.8 us
  transfers between devices with their start and end apart: 70, of which 24 were waited for; matrix products, arithmetic and copies ran while one was open for 6% of the time, Pallas kernels for 19%

profile of v1, /device:TPU:3, one launch (start us, length us, event | category | flops | bytes accessed | tf_op | source)
XLA Modules:
  0.0 790.6 jit_solution(2163482069750189103)
XLA Ops:
  20.4 67.5 %collective-permute-done.5.refs_1_ = bf16[2048,512]{1,0:T(8,128)(2,1)S(1)} collective-permute-done((bf16[2048,512]{1,0:T(8,128)(2,1)S(1)}, bf16[2048,512]{1,0:T(8,128)(2,1)S(1)}, u32[]{:S(2)}, u32[]{:S(2)}) %collective-permute-start.5) | collective-permute-done | bytes 2097184 | tf_op jit(solution)/shard_map/ppermute | solution.py:323
  87.9 3.4 hop_add.24
  92.6 18.1 %collective-permute-done.2.refs_1_ = bf16[2048,512]{1,0:T(8,128)(2,1)S(1)} collective-permute-done((bf16[2048,512]{1,0:T(8,128)(2,1)S(1)}, bf16[2048,512]{1,0:T(8,128)(2,1)S(1)}, u32[]{:S(2)}, u32[]{:S(2)}) %collective-permute-start.2) | collective-permute-done | bytes 2097184 | tf_op jit(solution)/shard_map/ppermute | solution.py:323
  110.7 3.4 hop_add.25
  115.3 35.5 %collective-permute-start.6 = (bf16[2048,1024]{1,0:T(8,128)(2,1)}, bf16[2048,1024]{1,0:T(8,128)(2,1)}, u32[]{:S(2)}, u32[]{:S(2)}) collective-permute-start(bf16[2048,1024]{1,0:T(8,128)(2,1)} %get-tuple-element.35), channel_id=1, source_target_pairs={{0,2},{2,0},{4,6},{6,4},{1,3},{3,1},{5,7},{7,5},{8,10},{10,8},{12,... | collective-permute-start | bytes 12582920 | tf_op jit(solution)/shard_map/ppermute | solution.py:333
  150.9 3.4 hop_add.26
  156.6 3.4 hop_add.27
  161.3 34.5 %collective-permute-start.9 = (bf16[2048,1024]{1,0:T(8,128)(2,1)}, bf16[2048,1024]{1,0:T(8,128)(2,1)}, u32[]{:S(2)}, u32[]{:S(2)}) collective-permute-start(bf16[2048,1024]{1,0:T(8,128)(2,1)} %get-tuple-element.39), channel_id=1, source_target_pairs={{0,2},{2,0},{4,6},{6,4},{1,3},{3,1},{5,7},{7,5},{8,10},{10,8},{12,... | collective-permute-start | bytes 12582920 | tf_op jit(solution)/shard_map/ppermute | solution.py:333
  195.9 4.2 hop_add.28
  203.5 4.1 hop_add.29
  209.1 33.6 %collective-permute-start.17 = (bf16[2048,1024]{1,0:T(8,128)(2,1)}, bf16[2048,1024]{1,0:T(8,128)(2,1)}, u32[]{:S(2)}, u32[]{:S(2)}) collective-permute-start(bf16[2048,1024]{1,0:T(8,128)(2,1)} %get-tuple-element.45), channel_id=1, source_target_pairs={{0,2},{2,0},{4,6},{6,4},{1,3},{3,1},{5,7},{7,5},{8,10},{10,8},{12,... | collective-permute-start | bytes 12582920 | tf_op jit(solution)/shard_map/ppermute | solution.py:333
  242.7 4.6 broadcast_select_fusion.5.refs_0_.refs_1_.refs_4_.refs_5_.refs_2_.refs_3_
  247.4 3.4 hop_add.30
  252.1 4.3 hop_add.31
  256.3 25.8 %collective-permute-start.25 = (bf16[2048,1024]{1,0:T(8,128)(2,1)}, bf16[2048,1024]{1,0:T(8,128)(2,1)}, u32[]{:S(2)}, u32[]{:S(2)}) collective-permute-start(bf16[2048,1024]{1,0:T(8,128)(2,1)} %get-tuple-element.51), channel_id=1, source_target_pairs={{0,2},{2,0},{4,6},{6,4},{1,3},{3,1},{5,7},{7,5},{8,10},{10,8},{12,... | collective-permute-start | bytes 12582920 | tf_op jit(solution)/shard_map/ppermute | solution.py:333
  282.1 2.4 broadcast_select_fusion.4.refs_2_.refs_3_.refs_6_.refs_7_.refs_4_.refs_5_
  284.6 14.5 %multiply.6 = (bf16[2,256,1536]{2,1,0:T(8,128)(2,1)S(1)}, f32[2,256,1536]{2,1,0:T(8,128)S(1)}) custom-call(s32[3]{0:T(128)S(1)} %pad_add_fusion.tab_ref, bf16[2048,1024]{1,0:T(8,128)(2,1)} %broadcast_select_fusion.5.refs_0_.refs_1_.refs_4_.refs_5_.refs_2_.refs_3_, bf16[2048,1024]{1,0:T(8,128)(2,1)} %broadcast_select_fusion.5.refs_0_.refs_1_.refs_4_.refs_5_.refs_2_.refs_3_, ...), custom_call_target="tpu_custom_call" | custom-call | flops 6442450944 | bytes 12582912 | tf_op jit(solution)/shard_map/multiply/pallas_call | solution.py:163
  303.1 15.6 %collective-permute-done.10 = bf16[2,256,1536]{2,1,0:T(8,128)(2,1)S(1)} collective-permute-done((bf16[2,256,1536]{2,1,0:T(8,128)(2,1)S(1)}, bf16[2,256,1536]{2,1,0:T(8,128)(2,1)S(1)}, u32[]{:S(2)}, u32[]{:S(2)}) %collective-permute-start.10) | collective-permute-done | bytes 1572896 | tf_op jit(solution)/shard_map/ppermute | solution.py:336
  319.2 11.3 %collective-permute-done.32.refs_1_ = bf16[2048,512]{1,0:T(8,128)(2,1)S(1)} collective-permute-done((bf16[2048,512]{1,0:T(8,128)(2,1)S(1)}, bf16[2048,512]{1,0:T(8,128)(2,1)S(1)}, u32[]{:S(2)}, u32[]{:S(2)}) %collective-permute-start.32) | collective-permute-done | bytes 2097184 | tf_op jit(solution)/shard_map/ppermute | solution.py:323
  330.5 3.4 hop_add.32
  333.9 18.7 %collective-permute-done.31.refs_1_ = bf16[2048,512]{1,0:T(8,128)(2,1)S(1)} collective-permute-done((bf16[2048,512]{1,0:T(8,128)(2,1)S(1)}, bf16[2048,512]{1,0:T(8,128)(2,1)S(1)}, u32[]{:S(2)}, u32[]{:S(2)}) %collective-permute-start.31) | collective-permute-done | bytes 2097184 | tf_op jit(solution)/shard_map/ppermute | solution.py:323
  352.6 4.0 hop_add.33
  359.3 4.8 broadcast_select_fusion.3.refs_0_.refs_1_.refs_6_.refs_7_
  364.1 2.5 broadcast_select_fusion.2.refs_0_.refs_1_.refs_8_.refs_9_.refs_2_.refs_3_
  366.6 18.2 %multiply.8 = (bf16[2,256,2048]{2,1,0:T(8,128)(2,1)}, f32[2,256,2048]{2,1,0:T(8,128)S(1)}) custom-call(s32[3]{0:T(128)S(1)} %pad_add_fusion.tab_ref, bf16[2048,1024]{1,0:T(8,128)(2,1)} %broadcast_select_fusion.2.refs_0_.refs_1_.refs_8_.refs_9_.refs_2_.refs_3_, bf16[2048,1024]{1,0:T(8,128)(2,1)} %broadcast_select_fusion.2.refs_0_.refs_1_.refs_8_.refs_9_.refs_2_.refs_3_, ...), custom_call_target="tpu_custom_call" | custom-call | flops 8589934592 | bytes 16777216 | tf_op jit(solution)/shard_map/multiply/pallas_call | solution.py:163
  385.1 2.8 fusion.5
  387.9 7.3 collective-permute-start.12
  395.3 11.2 %collective-permute-done.40.refs_1_ = bf16[2048,512]{1,0:T(8,128)(2,1)S(1)} collective-permute-done((bf16[2048,512]{1,0:T(8,128)(2,1)S(1)}, bf16[2048,512]{1,0:T(8,128)(2,1)S(1)}, u32[]{:S(2)}, u32[]{:S(2)}) %collective-permute-start.40) | collective-permute-done | bytes 2097184 | tf_op jit(solution)/shard_map/ppermute | solution.py:323
  406.4 3.4 hop_add.34.refs_2_
  409.9 3.5 hop_add.35
  413.3 14.5 %multiply.7 = (bf16[2,256,1536]{2,1,0:T(8,128)(2,1)}, f32[2,256,1536]{2,1,0:T(8,128)S(1)}) custom-call(s32[3]{0:T(128)S(1)} %pad_add_fusion.tab_ref, bf16[2048,1024]{1,0:T(8,128)(2,1)} %broadcast_select_fusion.3.refs_0_.refs_1_.refs_6_.refs_7_, bf16[2048,1024]{1,0:T(8,128)(2,1)} %broadcast_select_fusion.3.refs_0_.refs_1_.refs_6_.refs_7_, ...), custom_call_target="tpu_custom_call" | custom-call | flops 6442450944 | bytes 12582912 | tf_op jit(solution)/shard_map/multiply/pallas_call | solution.py:163
  429.8 2.6 fusion.7
  433.2 22.0 %multiply.9 = (bf16[2,256,2560]{2,1,0:T(8,128)(2,1)}, f32[2,256,2560]{2,1,0:T(8,128)}) custom-call(s32[3]{0:T(128)S(1)} %pad_add_fusion.tab_ref, bf16[2048,1024]{1,0:T(8,128)(2,1)S(1)} %broadcast_select_fusion.1.refs_0_.refs_1_.refs_10_.refs_11_.refs_4_.refs_5_, ...), custom_call_target="tpu_custom_call" | custom-call | flops 10737418240 | bytes 20971520 | tf_op jit(solution)/shard_map/multiply/pallas_call | solution.py:163
  462.2 3.7 fusion.1
  465.9 6.3 collective-permute-start.28
  472.2 4.7 broadcast_select_fusion.refs_0_.refs_1_.refs_6_.refs_7_
  477.0 13.9 %multiply.11 = (bf16[2,256,1536]{2,1,0:T(8,128)(2,1)S(1)}, f32[2,256,1536]{2,1,0:T(8,128)S(1)}) custom-call(s32[3]{0:T(128)S(1)} %pad_add_fusion.tab_ref, bf16[2048,1024]{1,0:T(8,128)(2,1)} %broadcast_select_fusion.refs_0_.refs_1_.refs_6_.refs_7_, bf16[2048,1024]{1,0:T(8,128)(2,1)} %broadcast_select_fusion.refs_0_.refs_1_.refs_6_.refs_7_, ...), custom_call_target="tpu_custom_call" | custom-call | flops 6442450944 | bytes 12582912 | tf_op jit(solution)/shard_map/multiply/pallas_call | solution.py:163
  491.9 3.6 collective-permute-done.34
  495.4 2.7 fusion.6
  498.7 13.9 %multiply.10 = (bf16[2,256,1536]{2,1,0:T(8,128)(2,1)S(1)}, f32[2,256,1536]{2,1,0:T(8,128)S(1)}) custom-call(s32[3]{0:T(128)S(1)} %pad_add_fusion.tab_ref, bf16[2048,1024]{1,0:T(8,128)(2,1)} %broadcast_select_fusion.refs_0_.refs_1_.refs_6_.refs_7_, bf16[2048,1024]{1,0:T(8,128)(2,1)} %broadcast_select_fusion.refs_0_.refs_1_.refs_6_.refs_7_, ...), custom_call_target="tpu_custom_call" | custom-call | flops 6442450944 | bytes 12582912 | tf_op jit(solution)/shard_map/multiply/pallas_call | solution.py:163
  515.6 4.6 collective-permute-start.20
  522.3 6.9 collective-permute-done.35
  532.0 17.5 %collective-permute-done.42 = bf16[2,256,1536]{2,1,0:T(8,128)(2,1)S(1)} collective-permute-done((bf16[2,256,1536]{2,1,0:T(8,128)(2,1)S(1)}, bf16[2,256,1536]{2,1,0:T(8,128)(2,1)S(1)}, u32[]{:S(2)}, u32[]{:S(2)}) %collective-permute-start.42) | collective-permute-done | bytes 1572896 | tf_op jit(solution)/shard_map/ppermute | solution.py:336
  549.5 7.8 collective-permute-start.36
  559.9 3.1 collective-permute-start.58
  570.6 12.9 %collective-permute-done.36 = bf16[256,2560]{1,0:T(8,128)(2,1)S(1)} collective-permute-done((bf16[256,2560]{1,0:T(8,128)(2,1)S(1)}, bf16[256,2560]{1,0:T(8,128)(2,1)S(1)}, u32[]{:S(2)}, u32[]{:S(2)}) %collective-permute-start.36) | collective-permute-done | bytes 1310752 | tf_op jit(solution)/shard_map/ppermute | solution.py:344
  585.3 5.3 collective-permute-start.44
  593.2 6.5 collective-permute-start.52
  600.5 14.3 %collective-permute-done.44 = bf16[256,1536]{1,0:T(8,128)(2,1)S(1)} collective-permute-done((bf16[256,1536]{1,0:T(8,128)(2,1)S(1)}, bf16[256,1536]{1,0:T(8,128)(2,1)S(1)}, u32[]{:S(2)}, u32[]{:S(2)}) %collective-permute-start.44) | collective-permute-done | bytes 786464 | tf_op jit(solution)/shard_map/ppermute | solution.py:344
  620.5 5.5 collective-permute-start.64
  626.0 4.1 collective-permute-start.59
  631.4 6.0 collective-permute-done.38
  640.9 8.4 %collective-permute-start.53 = (bf16[256,1536]{1,0:T(8,128)(2,1)S(1)}, bf16[256,1536]{1,0:T(8,128)(2,1)S(1)}, u32[]{:S(2)}, u32[]{:S(2)}) collective-permute-start(bf16[256,1536]{1,0:T(8,128)(2,1)S(1)} %get-tuple-element.74), channel_id=1, source_target_pairs={{2,0},{6,4},{3,1},{7,5},{10,8},{14,12},{11,9},{15,13},{18,16},{22,... | collective-permute-start | bytes 2359304 | tf_op jit(solution)/shard_map/ppermute | solution.py:349
  649.3 7.9 collective-permute-done.59.refs_13_
  657.2 6.0 collective-permute-start.65
  664.5 14.7 %collective-permute-done.51 = bf16[256,1536]{1,0:T(8,128)(2,1)S(1)} collective-permute-done((bf16[256,1536]{1,0:T(8,128)(2,1)S(1)}, bf16[256,1536]{1,0:T(8,128)(2,1)S(1)}, u32[]{:S(2)}, u32[]{:S(2)}) %collective-permute-start.51) | collective-permute-done | bytes 786464 | tf_op jit(solution)/shard_map/ppermute | solution.py:344
  680.3 15.7 %collective-permute-done.46 = bf16[256,1536]{1,0:T(8,128)(2,1)S(1)} collective-permute-done((bf16[256,1536]{1,0:T(8,128)(2,1)S(1)}, bf16[256,1536]{1,0:T(8,128)(2,1)S(1)}, u32[]{:S(2)}, u32[]{:S(2)}) %collective-permute-start.46) | collective-permute-done | bytes 786464 | tf_op jit(solution)/shard_map/ppermute | solution.py:344
  699.1 4.1 collective-permute-start.63
  707.9 20.5 %collective-permute-done.61.refs_15_ = bf16[256,2560]{1,0:T(8,128)(2,1)S(1)} collective-permute-done((bf16[256,2560]{1,0:T(8,128)(2,1)S(1)}, bf16[256,2560]{1,0:T(8,128)(2,1)S(1)}, u32[]{:S(2)}, u32[]{:S(2)}) %collective-permute-start.61) | collective-permute-done | bytes 1310752 | tf_op jit(solution)/shard_map/ppermute | solution.py:347
  728.4 2.8 collective-permute-start.67
  731.2 14.0 %collective-permute-done.63.refs_17_ = bf16[256,1536]{1,0:T(8,128)(2,1)S(1)} collective-permute-done((bf16[256,1536]{1,0:T(8,128)(2,1)S(1)}, bf16[256,1536]{1,0:T(8,128)(2,1)S(1)}, u32[]{:S(2)}, u32[]{:S(2)}) %collective-permute-start.63) | collective-permute-done | bytes 786464 | tf_op jit(solution)/shard_map/ppermute | solution.py:347
  746.5 3.0 collective-permute-start.69
  749.5 12.6 %collective-permute-done.62.refs_16_ = bf16[256,1536]{1,0:T(8,128)(2,1)S(1)} collective-permute-done((bf16[256,1536]{1,0:T(8,128)(2,1)S(1)}, bf16[256,1536]{1,0:T(8,128)(2,1)S(1)}, u32[]{:S(2)}, u32[]{:S(2)}) %collective-permute-start.62) | collective-permute-done | bytes 786464 | tf_op jit(solution)/shard_map/ppermute | solution.py:347
  765.6 24.8 %assemble.1 = (f32[1536,3072]{1,0:T(8,128)}, f32[1536,3072]{1,0:T(8,128)}) custom-call(s32[1]{0:T(128)} %bitcast.place_ref, f32[256,1536]{1,0:T(8,128)S(1)} %get-tuple-element.77.refs_0_, f32[256,1536]{1,0:T(8,128)S(1)} %get-tuple-element.75.refs_1_, f32[256,2048]{1,0:T(8,128)S(1)} %get-tuple-element.73.refs_2_, f32[256,2560]{1,0:T(8,128)} %get-tuple-element.71.refs_3_, ...), custom_call_target="tpu_custom_call" | custom-call | tf_op jit(solution)/shard_map/assemble/pallas_call | solution.py:249
  (152 shorter events, 99.3 us)
Async XLA Ops:
  15.4 72.5 %collective-permute-start.5 = (bf16[2048,512]{1,0:T(8,128)(2,1)S(1)}, bf16[2048,512]{1,0:T(8,128)(2,1)S(1)}, u32[]{:S(2)}, u32[]{:S(2)}) collective-permute-start(bf16[2048,512]{1,0:T(8,128)(2,1)S(1)} %hop_add.23), channel_id=1, source_target_pairs={{0,8},{26,18},{4,12},{30,22},{8,16},{18,10},{12,20},{22,14},{16,24... | collective-permute-start | bytes 6291464 | tf_op jit(solution)/shard_map/ppermute | solution.py:323
  19.1 91.6 %collective-permute-start.2 = (bf16[2048,512]{1,0:T(8,128)(2,1)S(1)}, bf16[2048,512]{1,0:T(8,128)(2,1)S(1)}, u32[]{:S(2)}, u32[]{:S(2)}) collective-permute-start(bf16[2048,512]{1,0:T(8,128)(2,1)S(1)} %hop_add.20), channel_id=1, source_target_pairs={{0,8},{26,18},{4,12},{30,22},{8,16},{18,10},{12,20},{22,14},{16,24... | collective-permute-start | bytes 6291464 | tf_op jit(solution)/shard_map/ppermute | solution.py:323
  91.3 59.6 %collective-permute-start.8 = (bf16[2048,512]{1,0:T(8,128)(2,1)S(1)}, bf16[2048,512]{1,0:T(8,128)(2,1)S(1)}, u32[]{:S(2)}, u32[]{:S(2)}) collective-permute-start(bf16[2048,512]{1,0:T(8,128)(2,1)S(1)} %get-tuple-element.37), channel_id=1, source_target_pairs={{0,8},{26,18},{4,12},{30,22},{8,16},{18,10},{12,20},{22,14},{16,24... | collective-permute-start | bytes 6291464 | tf_op jit(solution)/shard_map/ppermute | solution.py:323
  114.0 42.6 %collective-permute-start.7 = (bf16[2048,512]{1,0:T(8,128)(2,1)S(1)}, bf16[2048,512]{1,0:T(8,128)(2,1)S(1)}, u32[]{:S(2)}, u32[]{:S(2)}) collective-permute-start(bf16[2048,512]{1,0:T(8,128)(2,1)S(1)} %get-tuple-element.36), channel_id=1, source_target_pairs={{0,8},{26,18},{4,12},{30,22},{8,16},{18,10},{12,20},{22,14},{16,24... | collective-permute-start | bytes 6291464 | tf_op jit(solution)/shard_map/ppermute | solution.py:323
  115.3 127.4 %collective-permute-start.6 = (bf16[2048,1024]{1,0:T(8,128)(2,1)}, bf16[2048,1024]{1,0:T(8,128)(2,1)}, u32[]{:S(2)}, u32[]{:S(2)}) collective-permute-start(bf16[2048,1024]{1,0:T(8,128)(2,1)} %get-tuple-element.35), channel_id=1, source_target_pairs={{0,2},{2,0},{4,6},{6,4},{1,3},{3,1},{5,7},{7,5},{8,10},{10,8},{12,... | collective-permute-start | bytes 12582920 | tf_op jit(solution)/shard_map/ppermute | solution.py:333
  154.3 41.6 %collective-permute-start.16 = (bf16[2048,512]{1,0:T(8,128)(2,1)S(1)}, bf16[2048,512]{1,0:T(8,128)(2,1)S(1)}, u32[]{:S(2)}, u32[]{:S(2)}) collective-permute-start(bf16[2048,512]{1,0:T(8,128)(2,1)S(1)} %get-tuple-element.43), channel_id=1, source_target_pairs={{0,8},{26,18},{4,12},{30,22},{8,16},{18,10},{12,20},{22,14},{16,24... | collective-permute-start | bytes 6291464 | tf_op jit(solution)/shard_map/ppermute | solution.py:323
  160.0 43.5 %collective-permute-start.15 = (bf16[2048,512]{1,0:T(8,128)(2,1)S(1)}, bf16[2048,512]{1,0:T(8,128)(2,1)S(1)}, u32[]{:S(2)}, u32[]{:S(2)}) collective-permute-start(bf16[2048,512]{1,0:T(8,128)(2,1)S(1)} %get-tuple-element.42), channel_id=1, source_target_pairs={{0,8},{26,18},{4,12},{30,22},{8,16},{18,10},{12,20},{22,14},{16,24... | collective-permute-start | bytes 6291464 | tf_op jit(solution)/shard_map/ppermute | solution.py:323
  161.3 120.8 %collective-permute-start.9 = (bf16[2048,1024]{1,0:T(8,128)(2,1)}, bf16[2048,1024]{1,0:T(8,128)(2,1)}, u32[]{:S(2)}, u32[]{:S(2)}) collective-permute-start(bf16[2048,1024]{1,0:T(8,128)(2,1)} %get-tuple-element.39), channel_id=1, source_target_pairs={{0,2},{2,0},{4,6},{6,4},{1,3},{3,1},{5,7},{7,5},{8,10},{10,8},{12,... | collective-permute-start | bytes 12582920 | tf_op jit(solution)/shard_map/ppermute | solution.py:333
  200.0 47.3 %collective-permute-start.24 = (bf16[2048,512]{1,0:T(8,128)(2,1)}, bf16[2048,512]{1,0:T(8,128)(2,1)S(1)}, u32[]{:S(2)}, u32[]{:S(2)}) collective-permute-start(bf16[2048,512]{1,0:T(8,128)(2,1)} %get-tuple-element.49), channel_id=1, source_target_pairs={{0,8},{26,18},{4,12},{30,22},{8,16},{18,10},{12,20},{22,14},{16,24... | collective-permute-start | bytes 6291464 | tf_op jit(solution)/shard_map/ppermute | solution.py:323
  207.7 44.4 %collective-permute-start.23 = (bf16[2048,512]{1,0:T(8,128)(2,1)}, bf16[2048,512]{1,0:T(8,128)(2,1)}, u32[]{:S(2)}, u32[]{:S(2)}) collective-permute-start(bf16[2048,512]{1,0:T(8,128)(2,1)} %get-tuple-element.48), channel_id=1, source_target_pairs={{0,8},{26,18},{4,12},{30,22},{8,16},{18,10},{12,20},{22,14},{16,24... | collective-permute-start | bytes 6291464 | tf_op jit(solution)/shard_map/ppermute | solution.py:323
  209.1 150.1 %collective-permute-start.17 = (bf16[2048,1024]{1,0:T(8,128)(2,1)}, bf16[2048,1024]{1,0:T(8,128)(2,1)}, u32[]{:S(2)}, u32[]{:S(2)}) collective-permute-start(bf16[2048,1024]{1,0:T(8,128)(2,1)} %get-tuple-element.45), channel_id=1, source_target_pairs={{0,2},{2,0},{4,6},{6,4},{1,3},{3,1},{5,7},{7,5},{8,10},{10,8},{12,... | collective-permute-start | bytes 12582920 | tf_op jit(solution)/shard_map/ppermute | solution.py:333
  256.3 107.7 %collective-permute-start.25 = (bf16[2048,1024]{1,0:T(8,128)(2,1)}, bf16[2048,1024]{1,0:T(8,128)(2,1)}, u32[]{:S(2)}, u32[]{:S(2)}) collective-permute-start(bf16[2048,1024]{1,0:T(8,128)(2,1)} %get-tuple-element.51), channel_id=1, source_target_pairs={{0,2},{2,0},{4,6},{6,4},{1,3},{3,1},{5,7},{7,5},{8,10},{10,8},{12,... | collective-permute-start | bytes 12582920 | tf_op jit(solution)/shard_map/ppermute | solution.py:333
  299.1 19.6 %collective-permute-start.10 = (bf16[2,256,1536]{2,1,0:T(8,128)(2,1)S(1)}, bf16[2,256,1536]{2,1,0:T(8,128)(2,1)S(1)}, u32[]{:S(2)}, u32[]{:S(2)}) collective-permute-start(bf16[2,256,1536]{2,1,0:T(8,128)(2,1)S(1)} %get-tuple-element.41), channel_id=1, source_target_pairs={{0,4},{1,5},{2,3},{3,2},{4,0},{5,1},{6,7},{7,6},{8,12},{9,13},{10,... | collective-permute-start | bytes 4718600 | tf_op jit(solution)/shard_map/ppermute | solution.py:336
  300.4 30.1 %collective-permute-start.32 = (bf16[2048,512]{1,0:T(8,128)(2,1)S(1)}, bf16[2048,512]{1,0:T(8,128)(2,1)S(1)}, u32[]{:S(2)}, u32[]{:S(2)}) collective-permute-start(bf16[2048,512]{1,0:T(8,128)(2,1)S(1)} %copy-done.3), channel_id=1, source_target_pairs={{8,16},{18,10},{12,20},{22,14},{16,24},{10,2},{20,28},{14,6},{9,17... | collective-permute-start | bytes 6291464 | tf_op jit(solution)/shard_map/ppermute | solution.py:323
  301.8 50.7 %collective-permute-start.31 = (bf16[2048,512]{1,0:T(8,128)(2,1)S(1)}, bf16[2048,512]{1,0:T(8,128)(2,1)S(1)}, u32[]{:S(2)}, u32[]{:S(2)}) collective-permute-start(bf16[2048,512]{1,0:T(8,128)(2,1)S(1)} %get-tuple-element.54), channel_id=1, source_target_pairs={{8,16},{18,10},{12,20},{22,14},{16,24},{10,2},{20,28},{14,6},{9,17... | collective-permute-start | bytes 6291464 | tf_op jit(solution)/shard_map/ppermute | solution.py:323
  318.9 66.2 %collective-permute-start.11 = (bf16[256,1536]{1,0:T(8,128)(2,1)S(1)}, bf16[256,1536]{1,0:T(8,128)(2,1)}, u32[]{:S(2)}, u32[]{:S(2)}) collective-permute-start(bf16[256,1536]{1,0:T(8,128)(2,1)S(1)} %fusion.8), channel_id=1, source_target_pairs={{0,1},{1,0},{2,6},{3,7},{4,5},{5,4},{6,2},{7,3},{8,9},{9,8},{10,14... | collective-permute-start | bytes 2359304 | tf_op jit(solution)/shard_map/ppermute | solution.py:338
  356.6 53.3 %collective-permute-start.39 = (bf16[2048,512]{1,0:T(8,128)(2,1)}, bf16[2048,512]{1,0:T(8,128)(2,1)S(1)}, u32[]{:S(2)}, u32[]{:S(2)}) collective-permute-start(bf16[2048,512]{1,0:T(8,128)(2,1)} %get-tuple-element.60), channel_id=1, source_target_pairs={{16,24},{10,2},{20,28},{14,6},{17,25},{11,3},{21,29},{15,7}} | collective-permute-start | bytes 6291464 | tf_op jit(solution)/shard_map/ppermute | solution.py:323
  357.9 48.6 %collective-permute-start.40 = (bf16[2048,512]{1,0:T(8,128)(2,1)S(1)}, bf16[2048,512]{1,0:T(8,128)(2,1)S(1)}, u32[]{:S(2)}, u32[]{:S(2)}) collective-permute-start(bf16[2048,512]{1,0:T(8,128)(2,1)S(1)} %get-tuple-element.61), channel_id=1, source_target_pairs={{16,24},{10,2},{20,28},{14,6},{17,25},{11,3},{21,29},{15,7}} | collective-permute-start | bytes 6291464 | tf_op jit(solution)/shard_map/ppermute | solution.py:323
  359.2 73.5 %collective-permute-start.33 = (bf16[2048,1024]{1,0:T(8,128)(2,1)}, bf16[2048,1024]{1,0:T(8,128)(2,1)}, u32[]{:S(2)}, u32[]{:S(2)}) collective-permute-start(bf16[2048,1024]{1,0:T(8,128)(2,1)} %get-tuple-element.57), channel_id=1, source_target_pairs={{0,2},{2,0},{4,6},{6,4},{1,3},{3,1},{5,7},{7,5},{8,10},{10,8},{12,... | collective-permute-start | bytes 12582920 | tf_op jit(solution)/shard_map/ppermute | solution.py:333
  384.8 45.0 %collective-permute-start.26 = (bf16[2,256,2048]{2,1,0:T(8,128)(2,1)}, bf16[2,256,2048]{2,1,0:T(8,128)(2,1)}, u32[]{:S(2)}, u32[]{:S(2)}) collective-permute-start(bf16[2,256,2048]{2,1,0:T(8,128)(2,1)} %get-tuple-element.53), channel_id=1, source_target_pairs={{0,4},{1,5},{2,3},{3,2},{4,0},{5,1},{6,7},{7,6},{8,12},{9,13},{10,... | collective-permute-start | bytes 6291464 | tf_op jit(solution)/shard_map/ppermute | solution.py:336
  387.9 40.1 %collective-permute-start.12 = (bf16[256,1536]{1,0:T(8,128)(2,1)S(1)}, bf16[256,1536]{1,0:T(8,128)(2,1)}, u32[]{:S(2)}, u32[]{:S(2)}) collective-permute-start(bf16[256,1536]{1,0:T(8,128)(2,1)S(1)} %fusion.5), channel_id=1, source_target_pairs={{0,8},{24,16},{1,9},{25,17},{2,10},{26,18},{3,11},{27,19},{4,12},{... | collective-permute-start | bytes 2359304 | tf_op jit(solution)/shard_map/ppermute | solution.py:344
  413.3 58.9 %collective-permute-start.41 = (bf16[2048,1024]{1,0:T(8,128)(2,1)}, bf16[2048,1024]{1,0:T(8,128)(2,1)}, u32[]{:S(2)}, u32[]{:S(2)}) collective-permute-start(bf16[2048,1024]{1,0:T(8,128)(2,1)} %hop_add.35), channel_id=1, source_target_pairs={{0,2},{2,0},{4,6},{6,4},{1,3},{3,1},{5,7},{7,5},{8,10},{10,8},{12,... | collective-permute-start | bytes 12582920 | tf_op jit(solution)/shard_map/ppermute | solution.py:333
  427.8 30.8 %collective-permute-start.18 = (bf16[2,256,1536]{2,1,0:T(8,128)(2,1)}, bf16[2,256,1536]{2,1,0:T(8,128)(2,1)}, u32[]{:S(2)}, u32[]{:S(2)}) collective-permute-start(bf16[2,256,1536]{2,1,0:T(8,128)(2,1)} %get-tuple-element.47), channel_id=1, source_target_pairs={{0,4},{1,5},{2,3},{3,2},{4,0},{5,1},{6,7},{7,6},{8,12},{9,13},{10,... | collective-permute-start | bytes 4718600 | tf_op jit(solution)/shard_map/ppermute | solution.py:336
  428.0 32.8 %collective-permute-start.13 = (bf16[256,1536]{1,0:T(8,128)(2,1)}, bf16[256,1536]{1,0:T(8,128)(2,1)}, u32[]{:S(2)}, u32[]{:S(2)}) collective-permute-start(bf16[256,1536]{1,0:T(8,128)(2,1)} %collective-permute-done.12), channel_id=1, source_target_pairs={{8,16},{16,8},{9,17},{17,9},{10,18},{18,10},{11,19},{19,11},{12,20... | collective-permute-start | bytes 2359304 | tf_op jit(solution)/shard_map/ppermute | solution.py:344
  432.5 29.7 %collective-permute-start.27 = (bf16[256,2048]{1,0:T(8,128)(2,1)}, bf16[256,2048]{1,0:T(8,128)(2,1)}, u32[]{:S(2)}, u32[]{:S(2)}) collective-permute-start(bf16[256,2048]{1,0:T(8,128)(2,1)} %fusion.7), channel_id=1, source_target_pairs={{0,1},{1,0},{2,6},{3,7},{4,5},{5,4},{6,2},{7,3},{8,9},{9,8},{10,14... | collective-permute-start | bytes 3145736 | tf_op jit(solution)/shard_map/ppermute | solution.py:338
  455.2 40.2 %collective-permute-start.34 = (bf16[2,256,2560]{2,1,0:T(8,128)(2,1)}, bf16[2,256,2560]{2,1,0:T(8,128)(2,1)}, u32[]{:S(2)}, u32[]{:S(2)}) collective-permute-start(bf16[2,256,2560]{2,1,0:T(8,128)(2,1)} %get-tuple-element.59), channel_id=1, source_target_pairs={{0,4},{1,5},{2,3},{3,2},{4,0},{5,1},{6,7},{7,6},{8,12},{9,13},{10,... | collective-permute-start | bytes 7864328 | tf_op jit(solution)/shard_map/ppermute | solution.py:336
  460.9 51.7 %collective-permute-start.19 = (bf16[256,1536]{1,0:T(8,128)(2,1)}, bf16[256,1536]{1,0:T(8,128)(2,1)}, u32[]{:S(2)}, u32[]{:S(2)}) collective-permute-start(bf16[256,1536]{1,0:T(8,128)(2,1)} %fusion.9), channel_id=1, source_target_pairs={{0,1},{1,0},{2,6},{3,7},{4,5},{5,4},{6,2},{7,3},{8,9},{9,8},{10,14... | collective-permute-start | bytes 2359304 | tf_op jit(solution)/shard_map/ppermute | solution.py:338
  460.9 96.6 %collective-permute-start.14 = (bf16[256,1536]{1,0:T(8,128)(2,1)}, bf16[256,1536]{1,0:T(8,128)(2,1)}, u32[]{:S(2)}, u32[]{:S(2)}) collective-permute-start(bf16[256,1536]{1,0:T(8,128)(2,1)} %collective-permute-done.13), channel_id=1, source_target_pairs={{8,0},{16,24},{9,1},{17,25},{10,2},{18,26},{11,3},{19,27},{12,4},{... | collective-permute-start | bytes 2359304 | tf_op jit(solution)/shard_map/ppermute | solution.py:344
  465.9 49.7 %collective-permute-start.28 = (bf16[256,2048]{1,0:T(8,128)(2,1)}, bf16[256,2048]{1,0:T(8,128)(2,1)}, u32[]{:S(2)}, u32[]{:S(2)}) collective-permute-start(bf16[256,2048]{1,0:T(8,128)(2,1)} %fusion.1), channel_id=1, source_target_pairs={{0,8},{24,16},{1,9},{25,17},{2,10},{26,18},{3,11},{27,19},{4,12},{... | collective-permute-start | bytes 3145736 | tf_op jit(solution)/shard_map/ppermute | solution.py:344
  490.9 29.4 %collective-permute-start.47 = (bf16[2,256,1536]{2,1,0:T(8,128)(2,1)S(1)}, bf16[2,256,1536]{2,1,0:T(8,128)(2,1)}, u32[]{:S(2)}, u32[]{:S(2)}) collective-permute-start(bf16[2,256,1536]{2,1,0:T(8,128)(2,1)S(1)} %get-tuple-element.65), channel_id=1, source_target_pairs={{0,4},{1,5},{2,3},{3,2},{4,0},{5,1},{6,7},{7,6},{8,12},{9,13},{10,... | collective-permute-start | bytes 4718600 | tf_op jit(solution)/shard_map/ppermute | solution.py:336
  498.1 31.1 %collective-permute-start.35 = (bf16[256,2560]{1,0:T(8,128)(2,1)}, bf16[256,2560]{1,0:T(8,128)(2,1)}, u32[]{:S(2)}, u32[]{:S(2)}) collective-permute-start(bf16[256,2560]{1,0:T(8,128)(2,1)} %fusion.6), channel_id=1, source_target_pairs={{0,1},{1,0},{2,6},{3,7},{4,5},{5,4},{6,2},{7,3},{8,9},{9,8},{10,14... | collective-permute-start | bytes 3932168 | tf_op jit(solution)/shard_map/ppermute | solution.py:338
  512.6 36.9 %collective-permute-start.42 = (bf16[2,256,1536]{2,1,0:T(8,128)(2,1)S(1)}, bf16[2,256,1536]{2,1,0:T(8,128)(2,1)S(1)}, u32[]{:S(2)}, u32[]{:S(2)}) collective-permute-start(bf16[2,256,1536]{2,1,0:T(8,128)(2,1)S(1)} %get-tuple-element.63), channel_id=1, source_target_pairs={{0,4},{1,5},{2,3},{3,2},{4,0},{5,1},{6,7},{7,6},{8,12},{9,13},{10,... | collective-permute-start | bytes 4718600 | tf_op jit(solution)/shard_map/ppermute | solution.py:336
  515.6 44.3 %collective-permute-start.20 = (bf16[256,1536]{1,0:T(8,128)(2,1)S(1)}, bf16[256,1536]{1,0:T(8,128)(2,1)S(1)}, u32[]{:S(2)}, u32[]{:S(2)}) collective-permute-start(bf16[256,1536]{1,0:T(8,128)(2,1)S(1)} %fusion.4), channel_id=1, source_target_pairs={{0,8},{24,16},{1,9},{25,17},{2,10},{26,18},{3,11},{27,19},{4,12},{... | collective-permute-start | bytes 2359304 | tf_op jit(solution)/shard_map/ppermute | solution.py:344
  520.3 42.7 %collective-permute-start.29 = (bf16[256,2048]{1,0:T(8,128)(2,1)}, bf16[256,2048]{1,0:T(8,128)(2,1)S(1)}, u32[]{:S(2)}, u32[]{:S(2)}) collective-permute-start(bf16[256,2048]{1,0:T(8,128)(2,1)} %collective-permute-done.28), channel_id=1, source_target_pairs={{8,16},{16,8},{9,17},{17,9},{10,18},{18,10},{11,19},{19,11},{12,20... | collective-permute-start | bytes 3145736 | tf_op jit(solution)/shard_map/ppermute | solution.py:344
  529.2 34.5 %collective-permute-start.48 = (bf16[256,1536]{1,0:T(8,128)(2,1)S(1)}, bf16[256,1536]{1,0:T(8,128)(2,1)S(1)}, u32[]{:S(2)}, u32[]{:S(2)}) collective-permute-start(bf16[256,1536]{1,0:T(8,128)(2,1)S(1)} %fusion.11), channel_id=1, source_target_pairs={{0,1},{1,0},{2,6},{3,7},{4,5},{5,4},{6,2},{7,3},{8,9},{9,8},{10,14... | collective-permute-start | bytes 2359304 | tf_op jit(solution)/shard_map/ppermute | solution.py:338
  549.5 34.0 %collective-permute-start.36 = (bf16[256,2560]{1,0:T(8,128)(2,1)S(1)}, bf16[256,2560]{1,0:T(8,128)(2,1)S(1)}, u32[]{:S(2)}, u32[]{:S(2)}) collective-permute-start(bf16[256,2560]{1,0:T(8,128)(2,1)S(1)} %fusion), channel_id=1, source_target_pairs={{0,8},{24,16},{1,9},{25,17},{2,10},{26,18},{3,11},{27,19},{4,12},{... | collective-permute-start | bytes 3932168 | tf_op jit(solution)/shard_map/ppermute | solution.py:344
  557.5 11.2 %collective-permute-start.43 = (bf16[256,1536]{1,0:T(8,128)(2,1)S(1)}, bf16[256,1536]{1,0:T(8,128)(2,1)S(1)}, u32[]{:S(2)}, u32[]{:S(2)}) collective-permute-start(bf16[256,1536]{1,0:T(8,128)(2,1)S(1)} %fusion.10), channel_id=1, source_target_pairs={{0,1},{1,0},{2,6},{3,7},{4,5},{5,4},{6,2},{7,3},{8,9},{9,8},{10,14... | collective-permute-start | bytes 2359304 | tf_op jit(solution)/shard_map/ppermute | solution.py:338
  559.9 25.4 %collective-permute-start.58 = (bf16[256,1536]{1,0:T(8,128)(2,1)S(1)}, bf16[256,1536]{1,0:T(8,128)(2,1)S(1)}, u32[]{:S(2)}, u32[]{:S(2)}) collective-permute-start(bf16[256,1536]{1,0:T(8,128)(2,1)S(1)} %get-tuple-element.76), channel_id=1, source_target_pairs={{0,0},{1,4},{2,2},{3,6},{4,1},{5,5},{6,3},{7,7},{8,8},{9,12},{10,1... | collective-permute-start | bytes 2359304 | tf_op jit(solution)/shard_map/ppermute | solution.py:347
  563.0 27.6 %collective-permute-start.21 = (bf16[256,1536]{1,0:T(8,128)(2,1)S(1)}, bf16[256,1536]{1,0:T(8,128)(2,1)S(1)}, u32[]{:S(2)}, u32[]{:S(2)}) collective-permute-start(bf16[256,1536]{1,0:T(8,128)(2,1)S(1)} %collective-permute-done.20), channel_id=1, source_target_pairs={{8,16},{16,8},{9,17},{17,9},{10,18},{18,10},{11,19},{19,11},{12,20... | collective-permute-start | bytes 2359304 | tf_op jit(solution)/shard_map/ppermute | solution.py:344
  563.7 29.5 %collective-permute-start.30 = (bf16[256,2048]{1,0:T(8,128)(2,1)S(1)}, bf16[256,2048]{1,0:T(8,128)(2,1)S(1)}, u32[]{:S(2)}, u32[]{:S(2)}) collective-permute-start(bf16[256,2048]{1,0:T(8,128)(2,1)S(1)} %collective-permute-done.29), channel_id=1, source_target_pairs={{8,0},{16,24},{9,1},{17,25},{10,2},{18,26},{11,3},{19,27},{12,4},{... | collective-permute-start | bytes 3145736 | tf_op jit(solution)/shard_map/ppermute | solution.py:344
  568.7 31.0 %collective-permute-start.49 = (bf16[256,1536]{1,0:T(8,128)(2,1)S(1)}, bf16[256,1536]{1,0:T(8,128)(2,1)S(1)}, u32[]{:S(2)}, u32[]{:S(2)}) collective-permute-start(bf16[256,1536]{1,0:T(8,128)(2,1)S(1)} %fusion.2), channel_id=1, source_target_pairs={{0,8},{24,16},{1,9},{25,17},{2,10},{26,18},{3,11},{27,19},{4,12},{... | collective-permute-start | bytes 2359304 | tf_op jit(solution)/shard_map/ppermute | solution.py:344
  585.3 29.4 %collective-permute-start.44 = (bf16[256,1536]{1,0:T(8,128)(2,1)S(1)}, bf16[256,1536]{1,0:T(8,128)(2,1)S(1)}, u32[]{:S(2)}, u32[]{:S(2)}) collective-permute-start(bf16[256,1536]{1,0:T(8,128)(2,1)S(1)} %fusion.3), channel_id=1, source_target_pairs={{0,8},{24,16},{1,9},{25,17},{2,10},{26,18},{3,11},{27,19},{4,12},{... | collective-permute-start | bytes 2359304 | tf_op jit(solution)/shard_map/ppermute | solution.py:344
  590.6 27.3 %collective-permute-start.22 = (bf16[256,1536]{1,0:T(8,128)(2,1)S(1)}, bf16[256,1536]{1,0:T(8,128)(2,1)S(1)}, u32[]{:S(2)}, u32[]{:S(2)}) collective-permute-start(bf16[256,1536]{1,0:T(8,128)(2,1)S(1)} %collective-permute-done.21), channel_id=1, source_target_pairs={{8,0},{16,24},{9,1},{17,25},{10,2},{18,26},{11,3},{19,27},{12,4},{... | collective-permute-start | bytes 2359304 | tf_op jit(solution)/shard_map/ppermute | solution.py:344
  591.9 45.5 %collective-permute-start.38 = (bf16[256,2560]{1,0:T(8,128)(2,1)S(1)}, bf16[256,2560]{1,0:T(8,128)(2,1)S(1)}, u32[]{:S(2)}, u32[]{:S(2)}) collective-permute-start(bf16[256,2560]{1,0:T(8,128)(2,1)S(1)} %collective-permute-done.37), channel_id=1, source_target_pairs={{8,0},{16,24},{9,1},{17,25},{10,2},{18,26},{11,3},{19,27},{12,4},{... | collective-permute-start | bytes 3932168 | tf_op jit(solution)/shard_map/ppermute | solution.py:344
  593.2 27.3 %collective-permute-start.52 = (bf16[256,1536]{1,0:T(8,128)(2,1)S(1)}, bf16[256,1536]{1,0:T(8,128)(2,1)S(1)}, u32[]{:S(2)}, u32[]{:S(2)}) collective-permute-start(bf16[256,1536]{1,0:T(8,128)(2,1)S(1)} %get-tuple-element.76), channel_id=1, source_target_pairs={{2,0},{6,4},{3,1},{7,5},{10,8},{14,12},{11,9},{15,13},{18,16},{22,... | collective-permute-start | bytes 2359304 | tf_op jit(solution)/shard_map/ppermute | solution.py:349
  599.8 26.2 %collective-permute-start.50 = (bf16[256,1536]{1,0:T(8,128)(2,1)S(1)}, bf16[256,1536]{1,0:T(8,128)(2,1)S(1)}, u32[]{:S(2)}, u32[]{:S(2)}) collective-permute-start(bf16[256,1536]{1,0:T(8,128)(2,1)S(1)} %collective-permute-done.49), channel_id=1, source_target_pairs={{8,16},{16,8},{9,17},{17,9},{10,18},{18,10},{11,19},{19,11},{12,20... | collective-permute-start | bytes 2359304 | tf_op jit(solution)/shard_map/ppermute | solution.py:344
  614.8 15.3 %collective-permute-start.45 = (bf16[256,1536]{1,0:T(8,128)(2,1)S(1)}, bf16[256,1536]{1,0:T(8,128)(2,1)S(1)}, u32[]{:S(2)}, u32[]{:S(2)}) collective-permute-start(bf16[256,1536]{1,0:T(8,128)(2,1)S(1)} %collective-permute-done.44), channel_id=1, source_target_pairs={{8,16},{16,8},{9,17},{17,9},{10,18},{18,10},{11,19},{19,11},{12,20... | collective-permute-start | bytes 2359304 | tf_op jit(solution)/shard_map/ppermute | solution.py:344
  617.9 45.2 %collective-permute-start.60 = (bf16[256,2048]{1,0:T(8,128)(2,1)S(1)}, bf16[256,2048]{1,0:T(8,128)(2,1)S(1)}, u32[]{:S(2)}, u32[]{:S(2)}) collective-permute-start(bf16[256,2048]{1,0:T(8,128)(2,1)S(1)} %get-tuple-element.72), channel_id=1, source_target_pairs={{0,0},{1,4},{2,2},{3,6},{4,1},{5,5},{6,3},{7,7},{8,8},{9,12},{10,1... | collective-permute-start | bytes 3145736 | tf_op jit(solution)/shard_map/ppermute | solution.py:347
  620.5 20.4 %collective-permute-start.64 = (bf16[256,1536]{1,0:T(8,128)(2,1)S(1)}, bf16[256,1536]{1,0:T(8,128)(2,1)S(1)}, u32[]{:S(2)}, u32[]{:S(2)}) collective-permute-start(bf16[256,1536]{1,0:T(8,128)(2,1)S(1)} %collective-permute-done.58.refs_12_), channel_id=1, source_target_pairs={{0,2},{2,0},{4,6},{6,4},{1,3},{3,1},{5,7},{7,5},{8,10},{10,8},{12,... | collective-permute-start | bytes 2359304 | tf_op jit(solution)/shard_map/ppermute | solution.py:350
  626.0 31.2 %collective-permute-start.59 = (bf16[256,1536]{1,0:T(8,128)(2,1)S(1)}, bf16[256,1536]{1,0:T(8,128)(2,1)S(1)}, u32[]{:S(2)}, u32[]{:S(2)}) collective-permute-start(bf16[256,1536]{1,0:T(8,128)(2,1)S(1)} %get-tuple-element.74), channel_id=1, source_target_pairs={{0,0},{1,4},{2,2},{3,6},{4,1},{5,5},{6,3},{7,7},{8,8},{9,12},{10,1... | collective-permute-start | bytes 2359304 | tf_op jit(solution)/shard_map/ppermute | solution.py:347
  630.1 49.1 %collective-permute-start.51 = (bf16[256,1536]{1,0:T(8,128)(2,1)S(1)}, bf16[256,1536]{1,0:T(8,128)(2,1)S(1)}, u32[]{:S(2)}, u32[]{:S(2)}) collective-permute-start(bf16[256,1536]{1,0:T(8,128)(2,1)S(1)} %collective-permute-done.50), channel_id=1, source_target_pairs={{8,0},{16,24},{9,1},{17,25},{10,2},{18,26},{11,3},{19,27},{12,4},{... | collective-permute-start | bytes 2359304 | tf_op jit(solution)/shard_map/ppermute | solution.py:344
  637.4 58.6 %collective-permute-start.46 = (bf16[256,1536]{1,0:T(8,128)(2,1)S(1)}, bf16[256,1536]{1,0:T(8,128)(2,1)S(1)}, u32[]{:S(2)}, u32[]{:S(2)}) collective-permute-start(bf16[256,1536]{1,0:T(8,128)(2,1)S(1)} %collective-permute-done.45), channel_id=1, source_target_pairs={{8,0},{16,24},{9,1},{17,25},{10,2},{18,26},{11,3},{19,27},{12,4},{... | collective-permute-start | bytes 2359304 | tf_op jit(solution)/shard_map/ppermute | solution.py:344
  640.9 58.1 %collective-permute-start.53 = (bf16[256,1536]{1,0:T(8,128)(2,1)S(1)}, bf16[256,1536]{1,0:T(8,128)(2,1)S(1)}, u32[]{:S(2)}, u32[]{:S(2)}) collective-permute-start(bf16[256,1536]{1,0:T(8,128)(2,1)S(1)} %get-tuple-element.74), channel_id=1, source_target_pairs={{2,0},{6,4},{3,1},{7,5},{10,8},{14,12},{11,9},{15,13},{18,16},{22,... | collective-permute-start | bytes 2359304 | tf_op jit(solution)/shard_map/ppermute | solution.py:349
  657.2 46.0 %collective-permute-start.65 = (bf16[256,1536]{1,0:T(8,128)(2,1)S(1)}, bf16[256,1536]{1,0:T(8,128)(2,1)S(1)}, u32[]{:S(2)}, u32[]{:S(2)}) collective-permute-start(bf16[256,1536]{1,0:T(8,128)(2,1)S(1)} %collective-permute-done.59.refs_13_), channel_id=1, source_target_pairs={{0,2},{2,0},{4,6},{6,4},{1,3},{3,1},{5,7},{7,5},{8,10},{10,8},{12,... | collective-permute-start | bytes 2359304 | tf_op jit(solution)/shard_map/ppermute | solution.py:350
  663.2 41.3 %collective-permute-start.54 = (bf16[256,2048]{1,0:T(8,128)(2,1)S(1)}, bf16[256,2048]{1,0:T(8,128)(2,1)S(1)}, u32[]{:S(2)}, u32[]{:S(2)}) collective-permute-start(bf16[256,2048]{1,0:T(8,128)(2,1)S(1)} %get-tuple-element.72), channel_id=1, source_target_pairs={{0,2},{4,6},{1,3},{5,7},{8,10},{12,14},{9,11},{13,15},{16,18},{20,... | collective-permute-start | bytes 3145736 | tf_op jit(solution)/shard_map/ppermute | solution.py:349
  679.2 27.4 %collective-permute-start.66 = (bf16[256,2048]{1,0:T(8,128)(2,1)S(1)}, bf16[256,2048]{1,0:T(8,128)(2,1)S(1)}, u32[]{:S(2)}, u32[]{:S(2)}) collective-permute-start(bf16[256,2048]{1,0:T(8,128)(2,1)S(1)} %collective-permute-done.60.refs_14_), channel_id=1, source_target_pairs={{0,2},{2,0},{4,6},{6,4},{1,3},{3,1},{5,7},{7,5},{8,10},{10,8},{12,... | collective-permute-start | bytes 3145736 | tf_op jit(solution)/shard_map/ppermute | solution.py:350
  696.0 32.3 %collective-permute-start.61 = (bf16[256,2560]{1,0:T(8,128)(2,1)S(1)}, bf16[256,2560]{1,0:T(8,128)(2,1)S(1)}, u32[]{:S(2)}, u32[]{:S(2)}) collective-permute-start(bf16[256,2560]{1,0:T(8,128)(2,1)S(1)} %get-tuple-element.70), channel_id=1, source_target_pairs={{0,0},{1,4},{2,2},{3,6},{4,1},{5,5},{6,3},{7,7},{8,8},{9,12},{10,1... | collective-permute-start | bytes 3932168 | tf_op jit(solution)/shard_map/ppermute | solution.py:347
  699.1 46.2 %collective-permute-start.63 = (bf16[256,1536]{1,0:T(8,128)(2,1)S(1)}, bf16[256,1536]{1,0:T(8,128)(2,1)S(1)}, u32[]{:S(2)}, u32[]{:S(2)}) collective-permute-start(bf16[256,1536]{1,0:T(8,128)(2,1)S(1)} %get-tuple-element.66), channel_id=1, source_target_pairs={{0,0},{1,4},{2,2},{3,6},{4,1},{5,5},{6,3},{7,7},{8,8},{9,12},{10,1... | collective-permute-start | bytes 2359304 | tf_op jit(solution)/shard_map/ppermute | solution.py:347
  703.1 43.4 %collective-permute-start.57 = (bf16[256,1536]{1,0:T(8,128)(2,1)S(1)}, bf16[256,1536]{1,0:T(8,128)(2,1)S(1)}, u32[]{:S(2)}, u32[]{:S(2)}) collective-permute-start(bf16[256,1536]{1,0:T(8,128)(2,1)S(1)} %get-tuple-element.66), channel_id=1, source_target_pairs={{0,2},{4,6},{1,3},{5,7},{8,10},{12,14},{9,11},{13,15},{16,18},{20,... | collective-permute-start | bytes 2359304 | tf_op jit(solution)/shard_map/ppermute | solution.py:349
  704.5 57.6 %collective-permute-start.62 = (bf16[256,1536]{1,0:T(8,128)(2,1)S(1)}, bf16[256,1536]{1,0:T(8,128)(2,1)S(1)}, u32[]{:S(2)}, u32[]{:S(2)}) collective-permute-start(bf16[256,1536]{1,0:T(8,128)(2,1)S(1)} %get-tuple-element.68), channel_id=1, source_target_pairs={{0,0},{1,4},{2,2},{3,6},{4,1},{5,5},{6,3},{7,7},{8,8},{9,12},{10,1... | collective-permute-start | bytes 2359304 | tf_op jit(solution)/shard_map/ppermute | solution.py:347
  706.6 59.0 %collective-permute-start.55 = (bf16[256,2560]{1,0:T(8,128)(2,1)S(1)}, bf16[256,2560]{1,0:T(8,128)(2,1)S(1)}, u32[]{:S(2)}, u32[]{:S(2)}) collective-permute-start(bf16[256,2560]{1,0:T(8,128)(2,1)S(1)} %get-tuple-element.70), channel_id=1, source_target_pairs={{0,2},{4,6},{1,3},{5,7},{8,10},{12,14},{9,11},{13,15},{16,18},{20,... | collective-permute-start | bytes 3932168 | tf_op jit(solution)/shard_map/ppermute | solution.py:349
  728.4 37.2 %collective-permute-start.67 = (bf16[256,2560]{1,0:T(8,128)(2,1)S(1)}, bf16[256,2560]{1,0:T(8,128)(2,1)S(1)}, u32[]{:S(2)}, u32[]{:S(2)}) collective-permute-start(bf16[256,2560]{1,0:T(8,128)(2,1)S(1)} %collective-permute-done.61.refs_15_), channel_id=1, source_target_pairs={{0,2},{2,0},{4,6},{6,4},{1,3},{3,1},{5,7},{7,5},{8,10},{10,8},{12,... | collective-permute-start | bytes 3932168 | tf_op jit(solution)/shard_map/ppermute | solution.py:350
  745.2 18.5 %collective-permute-start.56 = (bf16[256,1536]{1,0:T(8,128)(2,1)S(1)}, bf16[256,1536]{1,0:T(8,128)(2,1)S(1)}, u32[]{:S(2)}, u32[]{:S(2)}) collective-permute-start(bf16[256,1536]{1,0:T(8,128)(2,1)S(1)} %get-tuple-element.68), channel_id=1, source_target_pairs={{0,2},{4,6},{1,3},{5,7},{8,10},{12,14},{9,11},{13,15},{16,18},{20,... | collective-permute-start | bytes 2359304 | tf_op jit(solution)/shard_map/ppermute | solution.py:349
  746.5 17.2 %collective-permute-start.69 = (bf16[256,1536]{1,0:T(8,128)(2,1)S(1)}, bf16[256,1536]{1,0:T(8,128)(2,1)S(1)}, u32[]{:S(2)}, u32[]{:S(2)}) collective-permute-start(bf16[256,1536]{1,0:T(8,128)(2,1)S(1)} %collective-permute-done.63.refs_17_), channel_id=1, source_target_pairs={{0,2},{2,0},{4,6},{6,4},{1,3},{3,1},{5,7},{7,5},{8,10},{10,8},{12,... | collective-permute-start | bytes 2359304 | tf_op jit(solution)/shard_map/ppermute | solution.py:350
  (18 other events, 254.9 us)

commit v2 on v1

--- a/solution.py
+++ b/solution.py
@@ -181,11 +181,19 @@
     )(tab, *operands)
 
 
-def assemble(place, own_me, own_other, mir_me, mir_other, statistic, width):
+def assemble(core, groups, blocks, own_me, own_other, mir_me, mir_other, statistic, width, made):
     half = width // 2
     rows, cols = statistic.shape
     here = rows // width
-    n_groups = len(GROUPS)
+    n = len(groups)
+    steps = max(len(b) for b in blocks)
+    tables = [
+        [b[min(k, len(b) - 1)][d] for d in range(2) for k in range(steps)] for b in blocks
+    ]
+    place = jnp.where(core == 0, jnp.array([0] + tables[0]), jnp.array([1] + tables[1])).astype(jnp.int32)
+
+    def at(place, k):
+        return place[1 + k], place[1 + steps + k]
 
     def own_at(g, j, i):
         start, first = GROUPS[g][0]
@@ -195,69 +203,69 @@
         return (j == start) & (i >= first) & (i <= final), jnp.clip(i - first, 0, final - first)
 
     def body(place_ref, *refs):
-        me = refs[:n_groups]
-        other = refs[n_groups : 2 * n_groups]
-        m_me = refs[2 * n_groups : 3 * n_groups]
-        m_other = refs[3 * n_groups : 4 * n_groups]
-        stat, gram_out, stat_out = refs[4 * n_groups :]
+        me, other, m_me, m_other = (refs[k * n : (k + 1) * n] for k in range(4))
+        stat = refs[4 * n]
+        gram_out, stat_out = refs[-2:]
+        r, i = at(place_ref, pl.program_id(0))
         core = place_ref[0]
-        j = core * here + pl.program_id(0)
-        i = pl.program_id(1)
-        for g in range(n_groups):
+        j = core * here + r
+        for k, g in enumerate(groups):
             lower, _ = own_at(g, j, i)
             upper, _ = own_at(g, i, j)
 
-            @pl.when(lower & (core == 0))
-            def _(g=g):
-                gram_out[:half, :] = me[g][...]
-                gram_out[half:, :] = other[g][...].astype(F32)
-
-            @pl.when(lower & (core != 0))
-            def _(g=g):
-                gram_out[:half, :] = other[g][...].astype(F32)
-                gram_out[half:, :] = me[g][...]
+            @pl.when(lower)
+            def _(k=k):
+                gram_out[pl.ds(pl.multiple_of(core * half, half), half), :] = me[k][...]
+                gram_out[pl.ds(pl.multiple_of((1 - core) * half, half), half), :] = other[k][...].astype(F32)
 
             @pl.when(upper & (i > j) & (core == 0))
-            def _(g=g):
-                gram_out[:, :half] = m_me[g][...].astype(F32).T
-                gram_out[:, half:] = m_other[g][...].astype(F32).T
+            def _(k=k):
+                gram_out[:, :half] = m_me[k][...].astype(F32).T
+                gram_out[:, half:] = m_other[k][...].astype(F32).T
 
             @pl.when(upper & (i > j) & (core != 0))
-            def _(g=g):
-                gram_out[:, :half] = m_other[g][...].astype(F32).T
-                gram_out[:, half:] = m_me[g][...].astype(F32).T
+            def _(k=k):
+                gram_out[:, :half] = m_other[k][...].astype(F32).T
+                gram_out[:, half:] = m_me[k][...].astype(F32).T
 
         stat_out[...] = 0.95 * stat[...] + 0.05 * gram_out[...]
 
     def low(g):
-        def index(r, c, place):
-            on, at = own_at(g, place[0] * here + r, c)
-            return (0, jnp.where(on, at, 0))
+        def index(k, place):
+            r, c = at(place, k)
+            on, where = own_at(g, place[0] * here + r, c)
+            return (0, jnp.where(on, where, 0))
 
         return pl.BlockSpec((half, width), index)
 
     def up(g):
-        def index(r, c, place):
+        def index(k, place):
+            r, c = at(place, k)
             j = place[0] * here + r
-            on, at = own_at(g, c, j)
-            return (0, jnp.where(on & (c > j), at, 0))
+            on, where = own_at(g, c, j)
+            return (0, jnp.where(on & (c > j), where, 1) - 1 if g == 0 else jnp.where(on & (c > j), where, 0))
 
         return pl.BlockSpec((half, width), index)
 
-    tile = pl.BlockSpec((width, width), lambda r, c, place: (r, c))
-    every = range(n_groups)
+    tile = pl.BlockSpec((width, width), lambda k, place: at(place, k))
+    tables = [[table[g] for g in groups] for table in (own_me, own_other, mir_me, mir_other)]
+    operands = [*tables[0], *tables[1], *tables[2], *tables[3], statistic]
+    in_specs = 2 * [low(g) for g in groups] + 2 * [up(g) for g in groups] + [tile]
+    alias = {}
+    if made is not None:
+        alias = {1 + len(operands): 0, 2 + len(operands): 1}
+        in_specs += [pl.BlockSpec(memory_space=pl.ANY)] * 2
+        operands += made
     return pl.pallas_call(
         body,
         grid_spec=pltpu.PrefetchScalarGridSpec(
-            num_scalar_prefetch=1,
-            grid=(here, cols // width),
-            in_specs=2 * [low(g) for g in every] + 2 * [up(g) for g in every] + [tile],
-            out_specs=[tile, tile],
+            num_scalar_prefetch=1, grid=(steps,), in_specs=in_specs, out_specs=[tile, tile]
         ),
         out_shape=[jax.ShapeDtypeStruct((rows, cols), F32)] * 2,
-        compiler_params=pltpu.CompilerParams(vmem_limit_bytes=28 * 1024 * 1024),
+        input_output_aliases=alias,
+        compiler_params=pltpu.CompilerParams(vmem_limit_bytes=50 * 1024 * 1024),
         name="assemble",
-    )(place, *own_me, *own_other, *mir_me, *mir_other, statistic)
+    )(place, *operands)
 
 
 def shards(grad_parts, statistic):
@@ -344,15 +352,24 @@
             cur = lax.ppermute(cur, "rep", sorted({(k, k + 1), (last - k, last - k - 1)}))
             total = total + cur.astype(F32)
         low = total.astype(BF16)
-        there = lax.ppermute(low, rc, mirror)
+        off = [k for k, (j, i) in enumerate(pairs) if j != i]
+        there = lax.ppermute(low[:, off[0] * width : (off[-1] + 1) * width], rc, mirror)
         owner = pairs[-1][0] // (STRIPS // 2)
         own_other.append(lax.ppermute(low, "row", [(i, i ^ 1) for i in range(rows_n) if i % 2 != owner]))
         mir_other.append(lax.ppermute(there, "row", swap_core))
         own_me.append(total)
         mir_me.append(there)
 
-    place = core[None].astype(jnp.int32)
-    return tuple(assemble(place, own_me, own_other, mir_me, mir_other, statistic, width))
+    here = STRIPS // 2
+    edge = STRIPS - 1
+    every = [[(k, i) for k in range(here) for i in range(STRIPS)] for _ in range(2)]
+    late = [[(k, i) for k, i in every[c] if max(c * here + k, i) == edge] for c in range(2)]
+    early = [[at for at in every[c] if at not in late[c]] for c in range(2)]
+    made = None
+    n_early = sum(pairs[0][0] < edge for pairs in GROUPS)
+    for groups, blocks in [(range(n_early), early), (range(n_early, len(GROUPS)), late)]:
+        made = assemble(core, groups, blocks, own_me, own_other, mir_me, mir_other, statistic, width, made)
+    return tuple(made)
 
 
 def solution(mesh):

time: 802 us -> 819 us (1.021)
  the two profiles are of different devices: /device:TPU:3 before, /device:TPU:5 now
where the time goes in v2:
time: 819 us; the launch traced here: 808 us
  waiting for transfers between devices  374 us (46%)
  starting transfers between devices  191 us (23%)
  Pallas kernels  190 us (23%)
  other arithmetic  45.3 us (6%)
    ppermute x16, waiting for transfers between devices, update(): recvs[s] = lax.ppermute(send, ('rep', 'row'), pairs)  198 us
    pallas_call x6, Pallas kernels, multiply(): pl.pallas_call(body, grid_spec=pltpu.PrefetchScalarGridSpec(num_scalar_pr...  96.4 us
    ppermute x18, waiting for transfers between devices, update(): lax.ppermute(cur, 'rep', sorted({(k, k + 1), (last - k, last - k - 1)}))  81.3 us
    ppermute x6, starting transfers between devices, update(): other = lax.ppermute(mine, 'row', swap_core)  68.6 us
    pallas_call x18, Pallas kernels, hop_add(): pl.pallas_call(body, grid_spec=pltpu.PrefetchScalarGridSpec(num_scalar_pr...  57.7 us
    ppermute x6, waiting for transfers between devices, update(): got = lax.ppermute(away, rc, phase_1)  51.6 us
    ppermute x18, starting transfers between devices, update(): lax.ppermute(cur, 'rep', sorted({(k, k + 1), (last - k, last - k - 1)}))  50.6 us
    pallas_call x2, Pallas kernels, assemble(): pl.pallas_call(body, grid_spec=pltpu.PrefetchScalarGridSpec(num_scalar_pr...  35.9 us
  transfers between devices with their start and end apart: 70, of which 23 were waited for; matrix products, arithmetic and copies ran while one was open for 6% of the time, Pallas kernels for 22%

profile of v2, /device:TPU:5, one launch (start us, length us, event | category | flops | bytes accessed | tf_op | source)
XLA Modules:
  0.0 807.6 jit_solution(8139976794846336037)
XLA Ops:
  20.4 67.5 %collective-permute-done.5.refs_1_ = bf16[2048,512]{1,0:T(8,128)(2,1)S(1)} collective-permute-done((bf16[2048,512]{1,0:T(8,128)(2,1)S(1)}, bf16[2048,512]{1,0:T(8,128)(2,1)S(1)}, u32[]{:S(2)}, u32[]{:S(2)}) %collective-permute-start.5) | collective-permute-done | bytes 2097184 | tf_op jit(solution)/shard_map/ppermute | solution.py:331
  87.9 3.4 hop_add.24
  92.6 18.1 %collective-permute-done.2.refs_1_ = bf16[2048,512]{1,0:T(8,128)(2,1)S(1)} collective-permute-done((bf16[2048,512]{1,0:T(8,128)(2,1)S(1)}, bf16[2048,512]{1,0:T(8,128)(2,1)S(1)}, u32[]{:S(2)}, u32[]{:S(2)}) %collective-permute-start.2) | collective-permute-done | bytes 2097184 | tf_op jit(solution)/shard_map/ppermute | solution.py:331
  110.7 3.4 hop_add.25
  115.3 35.5 %collective-permute-start.17 = (bf16[2048,1024]{1,0:T(8,128)(2,1)}, bf16[2048,1024]{1,0:T(8,128)(2,1)}, u32[]{:S(2)}, u32[]{:S(2)}) collective-permute-start(bf16[2048,1024]{1,0:T(8,128)(2,1)} %get-tuple-element.51), channel_id=1, source_target_pairs={{0,2},{2,0},{4,6},{6,4},{1,3},{3,1},{5,7},{7,5},{8,10},{10,8},{12,... | collective-permute-start | bytes 12582920 | tf_op jit(solution)/shard_map/ppermute | solution.py:341
  150.9 4.1 hop_add.26
  156.6 4.1 hop_add.27
  160.7 31.3 %collective-permute-start.18 = (bf16[2048,1024]{1,0:T(8,128)(2,1)}, bf16[2048,1024]{1,0:T(8,128)(2,1)}, u32[]{:S(2)}, u32[]{:S(2)}) collective-permute-start(bf16[2048,1024]{1,0:T(8,128)(2,1)} %get-tuple-element.52), channel_id=1, source_target_pairs={{0,2},{2,0},{4,6},{6,4},{1,3},{3,1},{5,7},{7,5},{8,10},{10,8},{12,... | collective-permute-start | bytes 12582920 | tf_op jit(solution)/shard_map/ppermute | solution.py:341
  194.6 25.1 %collective-permute-done.9.refs_1_ = bf16[2048,512]{1,0:T(8,128)(2,1)} collective-permute-done((bf16[2048,512]{1,0:T(8,128)(2,1)}, bf16[2048,512]{1,0:T(8,128)(2,1)}, u32[]{:S(2)}, u32[]{:S(2)}) %collective-permute-start.9) | collective-permute-done | bytes 2097184 | tf_op jit(solution)/shard_map/ppermute | solution.py:331
  219.8 4.5 hop_add.28
  224.2 17.9 %collective-permute-done.8.refs_1_ = bf16[2048,512]{1,0:T(8,128)(2,1)S(1)} collective-permute-done((bf16[2048,512]{1,0:T(8,128)(2,1)}, bf16[2048,512]{1,0:T(8,128)(2,1)S(1)}, u32[]{:S(2)}, u32[]{:S(2)}) %collective-permute-start.8) | collective-permute-done | bytes 2097184 | tf_op jit(solution)/shard_map/ppermute | solution.py:331
  242.1 3.7 hop_add.29
  246.4 2.6 broadcast_select_fusion.4.refs_2_.refs_3_.refs_0_.refs_1_.refs_4_.refs_5_
  252.6 14.5 %multiply.8 = (bf16[2,256,1536]{2,1,0:T(8,128)(2,1)S(1)}, f32[2,256,1536]{2,1,0:T(8,128)S(1)}) custom-call(s32[3]{0:T(128)S(1)} %pad_add_fusion.tab_ref, bf16[2048,1024]{1,0:T(8,128)(2,1)} %broadcast_select_fusion.4.refs_2_.refs_3_.refs_0_.refs_1_.refs_4_.refs_5_, bf16[2048,1024]{1,0:T(8,128)(2,1)} %broadcast_select_fusion.4.refs_2_.refs_3_.refs_0_.refs_1_.refs_4_.refs_5_, ...), custom_call_target="tpu_custom_call" | custom-call | flops 6442450944 | bytes 12582912 | tf_op jit(solution)/shard_map/multiply/pallas_call | solution.py:163
  270.0 16.7 %collective-permute-done.38 = bf16[2,256,1536]{2,1,0:T(8,128)(2,1)S(1)} collective-permute-done((bf16[2,256,1536]{2,1,0:T(8,128)(2,1)S(1)}, bf16[2,256,1536]{2,1,0:T(8,128)(2,1)S(1)}, u32[]{:S(2)}, u32[]{:S(2)}) %collective-permute-start.38) | collective-permute-done | bytes 1572896 | tf_op jit(solution)/shard_map/ppermute | solution.py:344
  289.2 9.5 %collective-permute-done.11.refs_1_ = bf16[2048,512]{1,0:T(8,128)(2,1)S(1)} collective-permute-done((bf16[2048,512]{1,0:T(8,128)(2,1)}, bf16[2048,512]{1,0:T(8,128)(2,1)S(1)}, u32[]{:S(2)}, u32[]{:S(2)}) %collective-permute-start.11) | collective-permute-done | bytes 2097184 | tf_op jit(solution)/shard_map/ppermute | solution.py:331
  298.7 3.4 hop_add.30
  303.6 17.2 %collective-permute-done.10.refs_1_ = bf16[2048,512]{1,0:T(8,128)(2,1)S(1)} collective-permute-done((bf16[2048,512]{1,0:T(8,128)(2,1)S(1)}, bf16[2048,512]{1,0:T(8,128)(2,1)S(1)}, u32[]{:S(2)}, u32[]{:S(2)}) %collective-permute-start.10) | collective-permute-done | bytes 2097184 | tf_op jit(solution)/shard_map/ppermute | solution.py:331
  320.8 3.6 hop_add.31
  329.5 6.5 collective-permute-start.40
  338.5 13.9 %multiply.9 = (bf16[2,256,1536]{2,1,0:T(8,128)(2,1)S(1)}, f32[2,256,1536]{2,1,0:T(8,128)S(1)}) custom-call(s32[3]{0:T(128)S(1)} %pad_add_fusion.tab_ref, bf16[2048,1024]{1,0:T(8,128)(2,1)} %broadcast_select_fusion.2.refs_6_.refs_7_.refs_0_.refs_1_, bf16[2048,1024]{1,0:T(8,128)(2,1)} %broadcast_select_fusion.2.refs_6_.refs_7_.refs_0_.refs_1_, ...), custom_call_target="tpu_custom_call" | custom-call | flops 6442450944 | bytes 12582912 | tf_op jit(solution)/shard_map/multiply/pallas_call | solution.py:163
  352.7 3.4 hop_add.32
  357.4 8.7 %collective-permute-done.12.refs_1_ = bf16[2048,512]{1,0:T(8,128)(2,1)S(1)} collective-permute-done((bf16[2048,512]{1,0:T(8,128)(2,1)S(1)}, bf16[2048,512]{1,0:T(8,128)(2,1)S(1)}, u32[]{:S(2)}, u32[]{:S(2)}) %collective-permute-start.12) | collective-permute-done | bytes 2097184 | tf_op jit(solution)/shard_map/ppermute | solution.py:331
  366.0 3.4 hop_add.33
  373.8 14.7 %collective-permute-done.15.refs_1_ = bf16[2048,512]{1,0:T(8,128)(2,1)S(1)} collective-permute-done((bf16[2048,512]{1,0:T(8,128)(2,1)S(1)}, bf16[2048,512]{1,0:T(8,128)(2,1)S(1)}, u32[]{:S(2)}, u32[]{:S(2)}) %collective-permute-start.15) | collective-permute-done | bytes 2097184 | tf_op jit(solution)/shard_map/ppermute | solution.py:331
  389.4 3.4 hop_add.34.refs_2_
  392.8 17.9 %collective-permute-done.14.refs_1_ = bf16[2048,512]{1,0:T(8,128)(2,1)S(1)} collective-permute-done((bf16[2048,512]{1,0:T(8,128)(2,1)S(1)}, bf16[2048,512]{1,0:T(8,128)(2,1)S(1)}, u32[]{:S(2)}, u32[]{:S(2)}) %collective-permute-start.14) | collective-permute-done | bytes 2097184 | tf_op jit(solution)/shard_map/ppermute | solution.py:331
  410.7 3.7 hop_add.35
  416.9 18.1 %multiply.10 = (bf16[2,256,2048]{2,1,0:T(8,128)(2,1)S(1)}, f32[2,256,2048]{2,1,0:T(8,128)S(1)}) custom-call(s32[3]{0:T(128)S(1)} %pad_add_fusion.tab_ref, bf16[2048,1024]{1,0:T(8,128)(2,1)} %broadcast_select_fusion.1.refs_2_.refs_3_.refs_0_.refs_1_.refs_8_.refs_9_, bf16[2048,1024]{1,0:T(8,128)(2,1)} %broadcast_select_fusion.1.refs_2_.refs_3_.refs_0_.refs_1_.refs_8_.refs_9_, ...), custom_call_target="tpu_custom_call" | custom-call | flops 8589934592 | bytes 16777216 | tf_op jit(solution)/shard_map/multiply/pallas_call | solution.py:163
  438.5 4.6 collective-permute-start.45
  443.5 22.0 %multiply.11 = (bf16[2,256,2560]{2,1,0:T(8,128)(2,1)}, f32[2,256,2560]{2,1,0:T(8,128)}) custom-call(s32[3]{0:T(128)S(1)} %pad_add_fusion.tab_ref, bf16[2048,1024]{1,0:T(8,128)(2,1)S(1)} %broadcast_select_fusion.refs_4_.refs_5_.refs_0_.refs_1_.refs_10_.refs_11_, bf16[2048,1024]{1,0:T(8,128)(2,1)S(1)} %broadcast_select_fusion.refs_4_.refs_5_.refs_0_.refs_1_.refs_10_.refs_11_, ...), custom_call_target="tpu_custom_call" | custom-call | flops 10737418240 | bytes 20971520 | tf_op jit(solution)/shard_map/multiply/pallas_call | solution.py:163
  469.1 3.1 fusion.7
  473.5 4.8 broadcast_select_fusion.5.refs_0_.refs_1_.refs_6_.refs_7_
  478.3 13.9 %multiply.7 = (bf16[2,256,1536]{2,1,0:T(8,128)(2,1)S(1)}, f32[2,256,1536]{2,1,0:T(8,128)S(1)}) custom-call(s32[3]{0:T(128)S(1)} %pad_add_fusion.tab_ref, bf16[2048,1024]{1,0:T(8,128)(2,1)} %broadcast_select_fusion.5.refs_0_.refs_1_.refs_6_.refs_7_, bf16[2048,1024]{1,0:T(8,128)(2,1)} %broadcast_select_fusion.5.refs_0_.refs_1_.refs_6_.refs_7_, ...), custom_call_target="tpu_custom_call" | custom-call | flops 6442450944 | bytes 12582912 | tf_op jit(solution)/shard_map/multiply/pallas_call | solution.py:163
  493.5 14.5 %collective-permute-done.53 = bf16[2,256,2560]{2,1,0:T(8,128)(2,1)} collective-permute-done((bf16[2,256,2560]{2,1,0:T(8,128)(2,1)}, bf16[2,256,2560]{2,1,0:T(8,128)(2,1)}, u32[]{:S(2)}, u32[]{:S(2)}) %collective-permute-start.53) | collective-permute-done | bytes 2621472 | tf_op jit(solution)/shard_map/ppermute | solution.py:344
  508.0 2.7 fusion.6
  511.9 13.9 %multiply.6 = (bf16[2,256,1536]{2,1,0:T(8,128)(2,1)S(1)}, f32[2,256,1536]{2,1,0:T(8,128)S(1)}) custom-call(s32[3]{0:T(128)S(1)} %pad_add_fusion.tab_ref, bf16[2048,1024]{1,0:T(8,128)(2,1)} %broadcast_select_fusion.5.refs_0_.refs_1_.refs_6_.refs_7_, bf16[2048,1024]{1,0:T(8,128)(2,1)} %broadcast_select_fusion.5.refs_0_.refs_1_.refs_6_.refs_7_, ...), custom_call_target="tpu_custom_call" | custom-call | flops 6442450944 | bytes 12582912 | tf_op jit(solution)/shard_map/multiply/pallas_call | solution.py:163
  527.9 3.6 collective-permute-done.27
  531.5 5.1 collective-permute-start.50
  536.8 5.0 collective-permute-done.54
  543.0 3.0 fusion
  546.0 15.5 %collective-permute-done.20 = bf16[2,256,1536]{2,1,0:T(8,128)(2,1)S(1)} collective-permute-done((bf16[2,256,1536]{2,1,0:T(8,128)(2,1)S(1)}, bf16[2,256,1536]{2,1,0:T(8,128)(2,1)S(1)}, u32[]{:S(2)}, u32[]{:S(2)}) %collective-permute-start.20) | collective-permute-done | bytes 1572896 | tf_op jit(solution)/shard_map/ppermute | solution.py:344
  561.4 5.1 collective-permute-start.55
  568.2 3.4 fusion.17
  578.0 5.9 collective-permute-start.29
  584.0 8.2 %collective-permute-done.55 = bf16[256,2560]{1,0:T(8,128)(2,1)S(1)} collective-permute-done((bf16[256,2560]{1,0:T(8,128)(2,1)S(1)}, bf16[256,2560]{1,0:T(8,128)(2,1)S(1)}, u32[]{:S(2)}, u32[]{:S(2)}) %collective-permute-start.55) | collective-permute-done | bytes 1310752 | tf_op jit(solution)/shard_map/ppermute | solution.py:352
  593.2 9.1 %collective-permute-start.22 = (bf16[256,1536]{1,0:T(8,128)(2,1)S(1)}, bf16[256,1536]{1,0:T(8,128)(2,1)S(1)}, u32[]{:S(2)}, u32[]{:S(2)}) collective-permute-start(bf16[256,1536]{1,0:T(8,128)(2,1)S(1)} %fusion.5), channel_id=1, source_target_pairs={{0,8},{24,16},{1,9},{25,17},{2,10},{26,18},{3,11},{27,19},{4,12},{... | collective-permute-start | bytes 2359304 | tf_op jit(solution)/shard_map/ppermute | solution.py:352
  605.1 4.8 collective-permute-start.58
  610.6 15.2 %collective-permute-done.22 = bf16[256,1536]{1,0:T(8,128)(2,1)S(1)} collective-permute-done((bf16[256,1536]{1,0:T(8,128)(2,1)S(1)}, bf16[256,1536]{1,0:T(8,128)(2,1)S(1)}, u32[]{:S(2)}, u32[]{:S(2)}) %collective-permute-start.22) | collective-permute-done | bytes 786464 | tf_op jit(solution)/shard_map/ppermute | solution.py:352
  626.5 3.0 fusion.16
  629.6 3.4 collective-permute-start.66
  637.2 3.0 collective-permute-start.63
  640.2 3.2 collective-permute-start.64
  644.7 13.4 %collective-permute-done.57 = bf16[256,2560]{1,0:T(8,128)(2,1)S(1)} collective-permute-done((bf16[256,2560]{1,0:T(8,128)(2,1)S(1)}, bf16[256,2560]{1,0:T(8,128)(2,1)S(1)}, u32[]{:S(2)}, u32[]{:S(2)}) %collective-permute-start.57) | collective-permute-done | bytes 1310752 | tf_op jit(solution)/shard_map/ppermute | solution.py:352
  661.8 3.7 collective-permute-start.67
  666.8 44.6 %collective-permute-done.24 = bf16[256,1536]{1,0:T(8,128)(2,1)S(1)} collective-permute-done((bf16[256,1536]{1,0:T(8,128)(2,1)S(1)}, bf16[256,1536]{1,0:T(8,128)(2,1)S(1)}, u32[]{:S(2)}, u32[]{:S(2)}) %collective-permute-start.24) | collective-permute-done | bytes 786464 | tf_op jit(solution)/shard_map/ppermute | solution.py:352
  711.3 3.0 collective-permute-start.65
  717.0 3.3 collective-permute-start.34
  723.4 3.0 collective-permute-start.35
  726.5 11.6 %collective-permute-done.65.refs_11_ = bf16[256,2048]{1,0:T(8,128)(2,1)S(1)} collective-permute-done((bf16[256,2048]{1,0:T(8,128)(2,1)S(1)}, bf16[256,2048]{1,0:T(8,128)(2,1)S(1)}, u32[]{:S(2)}, u32[]{:S(2)}) %collective-permute-start.65) | collective-permute-done | bytes 1048608 | tf_op jit(solution)/shard_map/ppermute | solution.py:356
  738.1 2.8 collective-permute-start.69
  742.2 23.9 %collective-permute-done.35.refs_5_ = bf16[256,1024]{1,0:T(8,128)(2,1)S(1)} collective-permute-done((bf16[256,1024]{1,0:T(8,128)(2,1)S(1)}, bf16[256,1024]{1,0:T(8,128)(2,1)S(1)}, u32[]{:S(2)}, u32[]{:S(2)}) %collective-permute-start.35) | collective-permute-done | bytes 524320 | tf_op jit(solution)/shard_map/ppermute | solution.py:356
  770.6 22.4 %assemble.2 = (f32[1536,3072]{1,0:T(8,128)}, f32[1536,3072]{1,0:T(8,128)}) custom-call(s32[31]{0:T(128)S(1)} %broadcast_select_fusion.6.place_ref, f32[256,1536]{1,0:T(8,128)} %get-tuple-element.77.refs_0_, f32[256,1536]{1,0:T(8,128)} %get-tuple-element.75.refs_1_, f32[256,2048]{1,0:T(8,128)} %get-tuple-element.73.refs_2_, ...), custom_call_target="tpu_custom_call" | custom-call | tf_op jit(solution)/shard_map/assemble/pallas_call | solution.py:259
  794.0 13.5 %assemble.3 = (f32[1536,3072]{1,0:T(8,128)}, f32[1536,3072]{1,0:T(8,128)}) custom-call(s32[17]{0:T(128)S(1)} %broadcast_select_fusion.7.place_ref, f32[256,1536]{1,0:T(8,128)} %get-tuple-element.81.refs_0_, f32[256,1536]{1,0:T(8,128)} %get-tuple-element.79.refs_1_, ...), custom_call_target="tpu_custom_call", output_to_operand_aliasing={{0}: (10, {}), {1}: (11, {})} | custom-call | tf_op jit(solution)/shard_map/assemble/pallas_call | solution.py:259
  (182 shorter events, 104.9 us)
Async XLA Ops:
  15.4 72.5 %collective-permute-start.5 = (bf16[2048,512]{1,0:T(8,128)(2,1)S(1)}, bf16[2048,512]{1,0:T(8,128)(2,1)S(1)}, u32[]{:S(2)}, u32[]{:S(2)}) collective-permute-start(bf16[2048,512]{1,0:T(8,128)(2,1)S(1)} %hop_add.23), channel_id=1, source_target_pairs={{0,8},{26,18},{4,12},{30,22},{8,16},{18,10},{12,20},{22,14},{16,24... | collective-permute-start | bytes 6291464 | tf_op jit(solution)/shard_map/ppermute | solution.py:331
  19.1 91.6 %collective-permute-start.2 = (bf16[2048,512]{1,0:T(8,128)(2,1)S(1)}, bf16[2048,512]{1,0:T(8,128)(2,1)S(1)}, u32[]{:S(2)}, u32[]{:S(2)}) collective-permute-start(bf16[2048,512]{1,0:T(8,128)(2,1)S(1)} %hop_add.20), channel_id=1, source_target_pairs={{0,8},{26,18},{4,12},{30,22},{8,16},{18,10},{12,20},{22,14},{16,24... | collective-permute-start | bytes 6291464 | tf_op jit(solution)/shard_map/ppermute | solution.py:331
  91.3 59.6 %collective-permute-start.7 = (bf16[2048,512]{1,0:T(8,128)(2,1)S(1)}, bf16[2048,512]{1,0:T(8,128)(2,1)S(1)}, u32[]{:S(2)}, u32[]{:S(2)}) collective-permute-start(bf16[2048,512]{1,0:T(8,128)(2,1)S(1)} %get-tuple-element.38), channel_id=1, source_target_pairs={{0,8},{26,18},{4,12},{30,22},{8,16},{18,10},{12,20},{22,14},{16,24... | collective-permute-start | bytes 6291464 | tf_op jit(solution)/shard_map/ppermute | solution.py:331
  114.1 42.6 %collective-permute-start.6 = (bf16[2048,512]{1,0:T(8,128)(2,1)S(1)}, bf16[2048,512]{1,0:T(8,128)(2,1)S(1)}, u32[]{:S(2)}, u32[]{:S(2)}) collective-permute-start(bf16[2048,512]{1,0:T(8,128)(2,1)S(1)} %get-tuple-element.37), channel_id=1, source_target_pairs={{0,8},{26,18},{4,12},{30,22},{8,16},{18,10},{12,20},{22,14},{16,24... | collective-permute-start | bytes 6291464 | tf_op jit(solution)/shard_map/ppermute | solution.py:331
  115.3 131.0 %collective-permute-start.17 = (bf16[2048,1024]{1,0:T(8,128)(2,1)}, bf16[2048,1024]{1,0:T(8,128)(2,1)}, u32[]{:S(2)}, u32[]{:S(2)}) collective-permute-start(bf16[2048,1024]{1,0:T(8,128)(2,1)} %get-tuple-element.51), channel_id=1, source_target_pairs={{0,2},{2,0},{4,6},{6,4},{1,3},{3,1},{5,7},{7,5},{8,10},{10,8},{12,... | collective-permute-start | bytes 12582920 | tf_op jit(solution)/shard_map/ppermute | solution.py:341
  160.7 88.3 %collective-permute-start.18 = (bf16[2048,1024]{1,0:T(8,128)(2,1)}, bf16[2048,1024]{1,0:T(8,128)(2,1)}, u32[]{:S(2)}, u32[]{:S(2)}) collective-permute-start(bf16[2048,1024]{1,0:T(8,128)(2,1)} %get-tuple-element.52), channel_id=1, source_target_pairs={{0,2},{2,0},{4,6},{6,4},{1,3},{3,1},{5,7},{7,5},{8,10},{10,8},{12,... | collective-permute-start | bytes 12582920 | tf_op jit(solution)/shard_map/ppermute | solution.py:341
  191.9 27.8 %collective-permute-start.9 = (bf16[2048,512]{1,0:T(8,128)(2,1)}, bf16[2048,512]{1,0:T(8,128)(2,1)}, u32[]{:S(2)}, u32[]{:S(2)}) collective-permute-start(bf16[2048,512]{1,0:T(8,128)(2,1)} %get-tuple-element.41), channel_id=1, source_target_pairs={{0,8},{26,18},{4,12},{30,22},{8,16},{18,10},{12,20},{22,14},{16,24... | collective-permute-start | bytes 6291464 | tf_op jit(solution)/shard_map/ppermute | solution.py:331
  193.2 48.9 %collective-permute-start.8 = (bf16[2048,512]{1,0:T(8,128)(2,1)}, bf16[2048,512]{1,0:T(8,128)(2,1)S(1)}, u32[]{:S(2)}, u32[]{:S(2)}) collective-permute-start(bf16[2048,512]{1,0:T(8,128)(2,1)} %get-tuple-element.40), channel_id=1, source_target_pairs={{0,8},{26,18},{4,12},{30,22},{8,16},{18,10},{12,20},{22,14},{16,24... | collective-permute-start | bytes 6291464 | tf_op jit(solution)/shard_map/ppermute | solution.py:331
  245.8 90.1 %collective-permute-start.19 = (bf16[2048,1024]{1,0:T(8,128)(2,1)}, bf16[2048,1024]{1,0:T(8,128)(2,1)}, u32[]{:S(2)}, u32[]{:S(2)}) collective-permute-start(bf16[2048,1024]{1,0:T(8,128)(2,1)} %get-tuple-element.53), channel_id=1, source_target_pairs={{0,2},{2,0},{4,6},{6,4},{1,3},{3,1},{5,7},{7,5},{8,10},{10,8},{12,... | collective-permute-start | bytes 12582920 | tf_op jit(solution)/shard_map/ppermute | solution.py:341
  267.1 19.6 %collective-permute-start.38 = (bf16[2,256,1536]{2,1,0:T(8,128)(2,1)S(1)}, bf16[2,256,1536]{2,1,0:T(8,128)(2,1)S(1)}, u32[]{:S(2)}, u32[]{:S(2)}) collective-permute-start(bf16[2,256,1536]{2,1,0:T(8,128)(2,1)S(1)} %get-tuple-element.61), channel_id=1, source_target_pairs={{0,4},{1,5},{2,3},{3,2},{4,0},{5,1},{6,7},{7,6},{8,12},{9,13},{10,... | collective-permute-start | bytes 4718600 | tf_op jit(solution)/shard_map/ppermute | solution.py:344
  267.4 31.3 %collective-permute-start.11 = (bf16[2048,512]{1,0:T(8,128)(2,1)}, bf16[2048,512]{1,0:T(8,128)(2,1)S(1)}, u32[]{:S(2)}, u32[]{:S(2)}) collective-permute-start(bf16[2048,512]{1,0:T(8,128)(2,1)} %get-tuple-element.44), channel_id=1, source_target_pairs={{0,8},{26,18},{4,12},{30,22},{8,16},{18,10},{12,20},{22,14},{16,24... | collective-permute-start | bytes 6291464 | tf_op jit(solution)/shard_map/ppermute | solution.py:331
  268.7 52.1 %collective-permute-start.10 = (bf16[2048,512]{1,0:T(8,128)(2,1)S(1)}, bf16[2048,512]{1,0:T(8,128)(2,1)S(1)}, u32[]{:S(2)}, u32[]{:S(2)}) collective-permute-start(bf16[2048,512]{1,0:T(8,128)(2,1)S(1)} %get-tuple-element.43), channel_id=1, source_target_pairs={{0,8},{26,18},{4,12},{30,22},{8,16},{18,10},{12,20},{22,14},{16,24... | collective-permute-start | bytes 6291464 | tf_op jit(solution)/shard_map/ppermute | solution.py:331
  288.0 39.0 %collective-permute-start.39 = (bf16[256,1536]{1,0:T(8,128)(2,1)}, bf16[256,1536]{1,0:T(8,128)(2,1)}, u32[]{:S(2)}, u32[]{:S(2)}) collective-permute-start(bf16[256,1536]{1,0:T(8,128)(2,1)} %fusion.10), channel_id=1, source_target_pairs={{0,1},{1,0},{2,6},{3,7},{4,5},{5,4},{6,2},{7,3},{8,9},{9,8},{10,14... | collective-permute-start | bytes 2359304 | tf_op jit(solution)/shard_map/ppermute | solution.py:346
  302.1 50.6 %collective-permute-start.13 = (bf16[2048,512]{1,0:T(8,128)(2,1)S(1)}, bf16[2048,512]{1,0:T(8,128)(2,1)S(1)}, u32[]{:S(2)}, u32[]{:S(2)}) collective-permute-start(bf16[2048,512]{1,0:T(8,128)(2,1)S(1)} %get-tuple-element.47), channel_id=1, source_target_pairs={{8,16},{18,10},{12,20},{22,14},{16,24},{10,2},{20,28},{14,6},{9,17... | collective-permute-start | bytes 6291464 | tf_op jit(solution)/shard_map/ppermute | solution.py:331
  324.4 41.6 %collective-permute-start.12 = (bf16[2048,512]{1,0:T(8,128)(2,1)S(1)}, bf16[2048,512]{1,0:T(8,128)(2,1)S(1)}, u32[]{:S(2)}, u32[]{:S(2)}) collective-permute-start(bf16[2048,512]{1,0:T(8,128)(2,1)S(1)} %get-tuple-element.46), channel_id=1, source_target_pairs={{8,16},{18,10},{12,20},{22,14},{16,24},{10,2},{20,28},{14,6},{9,17... | collective-permute-start | bytes 6291464 | tf_op jit(solution)/shard_map/ppermute | solution.py:331
  325.7 88.7 %collective-permute-start.25 = (bf16[2048,1024]{1,0:T(8,128)(2,1)}, bf16[2048,1024]{1,0:T(8,128)(2,1)}, u32[]{:S(2)}, u32[]{:S(2)}) collective-permute-start(bf16[2048,1024]{1,0:T(8,128)(2,1)} %get-tuple-element.56), channel_id=1, source_target_pairs={{0,2},{2,0},{4,6},{6,4},{1,3},{3,1},{5,7},{7,5},{8,10},{10,8},{12,... | collective-permute-start | bytes 12582920 | tf_op jit(solution)/shard_map/ppermute | solution.py:341
  329.5 41.2 %collective-permute-start.40 = (bf16[256,1536]{1,0:T(8,128)(2,1)}, bf16[256,1536]{1,0:T(8,128)(2,1)}, u32[]{:S(2)}, u32[]{:S(2)}) collective-permute-start(bf16[256,1536]{1,0:T(8,128)(2,1)} %fusion.3), channel_id=1, source_target_pairs={{0,8},{24,16},{1,9},{25,17},{2,10},{26,18},{3,11},{27,19},{4,12},{... | collective-permute-start | bytes 2359304 | tf_op jit(solution)/shard_map/ppermute | solution.py:352
  352.4 19.6 %collective-permute-start.43 = (bf16[2,256,1536]{2,1,0:T(8,128)(2,1)S(1)}, bf16[2,256,1536]{2,1,0:T(8,128)(2,1)S(1)}, u32[]{:S(2)}, u32[]{:S(2)}) collective-permute-start(bf16[2,256,1536]{2,1,0:T(8,128)(2,1)S(1)} %get-tuple-element.63), channel_id=1, source_target_pairs={{0,4},{1,5},{2,3},{3,2},{4,0},{5,1},{6,7},{7,6},{8,12},{9,13},{10,... | collective-permute-start | bytes 4718600 | tf_op jit(solution)/shard_map/ppermute | solution.py:344
  356.1 32.4 %collective-permute-start.15 = (bf16[2048,512]{1,0:T(8,128)(2,1)S(1)}, bf16[2048,512]{1,0:T(8,128)(2,1)S(1)}, u32[]{:S(2)}, u32[]{:S(2)}) collective-permute-start(bf16[2048,512]{1,0:T(8,128)(2,1)S(1)} %get-tuple-element.50), channel_id=1, source_target_pairs={{16,24},{10,2},{20,28},{14,6},{17,25},{11,3},{21,29},{15,7}} | collective-permute-start | bytes 6291464 | tf_op jit(solution)/shard_map/ppermute | solution.py:331
  369.4 41.3 %collective-permute-start.14 = (bf16[2048,512]{1,0:T(8,128)(2,1)S(1)}, bf16[2048,512]{1,0:T(8,128)(2,1)S(1)}, u32[]{:S(2)}, u32[]{:S(2)}) collective-permute-start(bf16[2048,512]{1,0:T(8,128)(2,1)S(1)} %get-tuple-element.49), channel_id=1, source_target_pairs={{16,24},{10,2},{20,28},{14,6},{17,25},{11,3},{21,29},{15,7}} | collective-permute-start | bytes 6291464 | tf_op jit(solution)/shard_map/ppermute | solution.py:331
  370.7 72.4 %collective-permute-start.26 = (bf16[2048,1024]{1,0:T(8,128)(2,1)}, bf16[2048,1024]{1,0:T(8,128)(2,1)}, u32[]{:S(2)}, u32[]{:S(2)}) collective-permute-start(bf16[2048,1024]{1,0:T(8,128)(2,1)} %get-tuple-element.57), channel_id=1, source_target_pairs={{0,2},{2,0},{4,6},{6,4},{1,3},{3,1},{5,7},{7,5},{8,10},{10,8},{12,... | collective-permute-start | bytes 12582920 | tf_op jit(solution)/shard_map/ppermute | solution.py:341
  372.1 93.8 %collective-permute-start.41 = (bf16[256,1536]{1,0:T(8,128)(2,1)}, bf16[256,1536]{1,0:T(8,128)(2,1)}, u32[]{:S(2)}, u32[]{:S(2)}) collective-permute-start(bf16[256,1536]{1,0:T(8,128)(2,1)} %collective-permute-done.40), channel_id=1, source_target_pairs={{8,16},{16,8},{9,17},{17,9},{10,18},{18,10},{11,19},{19,11},{12,20... | collective-permute-start | bytes 2359304 | tf_op jit(solution)/shard_map/ppermute | solution.py:352
  388.5 49.7 %collective-permute-start.44 = (bf16[256,1536]{1,0:T(8,128)(2,1)S(1)}, bf16[256,1536]{1,0:T(8,128)(2,1)S(1)}, u32[]{:S(2)}, u32[]{:S(2)}) collective-permute-start(bf16[256,1536]{1,0:T(8,128)(2,1)S(1)} %fusion.11), channel_id=1, source_target_pairs={{0,1},{1,0},{2,6},{3,7},{4,5},{5,4},{6,2},{7,3},{8,9},{9,8},{10,14... | collective-permute-start | bytes 2359304 | tf_op jit(solution)/shard_map/ppermute | solution.py:346
  414.4 59.1 %collective-permute-start.16 = (bf16[2048,1024]{1,0:T(8,128)(2,1)}, bf16[2048,1024]{1,0:T(8,128)(2,1)}, u32[]{:S(2)}, u32[]{:S(2)}) collective-permute-start(bf16[2048,1024]{1,0:T(8,128)(2,1)} %hop_add.35), channel_id=1, source_target_pairs={{0,2},{2,0},{4,6},{6,4},{1,3},{3,1},{5,7},{7,5},{8,10},{10,8},{12,... | collective-permute-start | bytes 12582920 | tf_op jit(solution)/shard_map/ppermute | solution.py:341
  437.0 32.1 %collective-permute-start.48 = (bf16[2,256,2048]{2,1,0:T(8,128)(2,1)S(1)}, bf16[2,256,2048]{2,1,0:T(8,128)(2,1)}, u32[]{:S(2)}, u32[]{:S(2)}) collective-permute-start(bf16[2,256,2048]{2,1,0:T(8,128)(2,1)S(1)} %get-tuple-element.65), channel_id=1, source_target_pairs={{0,4},{1,5},{2,3},{3,2},{4,0},{5,1},{6,7},{7,6},{8,12},{9,13},{10,... | collective-permute-start | bytes 6291464 | tf_op jit(solution)/shard_map/ppermute | solution.py:344
  438.5 28.6 %collective-permute-start.45 = (bf16[256,1536]{1,0:T(8,128)(2,1)S(1)}, bf16[256,1536]{1,0:T(8,128)(2,1)}, u32[]{:S(2)}, u32[]{:S(2)}) collective-permute-start(bf16[256,1536]{1,0:T(8,128)(2,1)S(1)} %fusion.2), channel_id=1, source_target_pairs={{0,8},{24,16},{1,9},{25,17},{2,10},{26,18},{3,11},{27,19},{4,12},{... | collective-permute-start | bytes 2359304 | tf_op jit(solution)/shard_map/ppermute | solution.py:352
  465.6 42.4 %collective-permute-start.53 = (bf16[2,256,2560]{2,1,0:T(8,128)(2,1)}, bf16[2,256,2560]{2,1,0:T(8,128)(2,1)}, u32[]{:S(2)}, u32[]{:S(2)}) collective-permute-start(bf16[2,256,2560]{2,1,0:T(8,128)(2,1)} %get-tuple-element.67), channel_id=1, source_target_pairs={{0,4},{1,5},{2,3},{3,2},{4,0},{5,1},{6,7},{7,6},{8,12},{9,13},{10,... | collective-permute-start | bytes 7864328 | tf_op jit(solution)/shard_map/ppermute | solution.py:344
  465.9 101.0 %collective-permute-start.42 = (bf16[256,1536]{1,0:T(8,128)(2,1)}, bf16[256,1536]{1,0:T(8,128)(2,1)}, u32[]{:S(2)}, u32[]{:S(2)}) collective-permute-start(bf16[256,1536]{1,0:T(8,128)(2,1)} %collective-permute-done.41), channel_id=1, source_target_pairs={{8,0},{16,24},{9,1},{17,25},{10,2},{18,26},{11,3},{19,27},{12,4},{... | collective-permute-start | bytes 2359304 | tf_op jit(solution)/shard_map/ppermute | solution.py:352
  467.2 104.5 %collective-permute-start.46 = (bf16[256,1536]{1,0:T(8,128)(2,1)}, bf16[256,1536]{1,0:T(8,128)(2,1)}, u32[]{:S(2)}, u32[]{:S(2)}) collective-permute-start(bf16[256,1536]{1,0:T(8,128)(2,1)} %collective-permute-done.45), channel_id=1, source_target_pairs={{8,16},{16,8},{9,17},{17,9},{10,18},{18,10},{11,19},{19,11},{12,20... | collective-permute-start | bytes 2359304 | tf_op jit(solution)/shard_map/ppermute | solution.py:352
  472.3 53.5 %collective-permute-start.49 = (bf16[256,2048]{1,0:T(8,128)(2,1)}, bf16[256,2048]{1,0:T(8,128)(2,1)S(1)}, u32[]{:S(2)}, u32[]{:S(2)}) collective-permute-start(bf16[256,2048]{1,0:T(8,128)(2,1)} %fusion.7), channel_id=1, source_target_pairs={{0,1},{1,0},{2,6},{3,7},{4,5},{5,4},{6,2},{7,3},{8,9},{9,8},{10,14... | collective-permute-start | bytes 3145736 | tf_op jit(solution)/shard_map/ppermute | solution.py:346
  492.2 39.3 %collective-permute-start.27 = (bf16[2,256,1536]{2,1,0:T(8,128)(2,1)S(1)}, bf16[2,256,1536]{2,1,0:T(8,128)(2,1)S(1)}, u32[]{:S(2)}, u32[]{:S(2)}) collective-permute-start(bf16[2,256,1536]{2,1,0:T(8,128)(2,1)S(1)} %get-tuple-element.59), channel_id=1, source_target_pairs={{0,4},{1,5},{2,3},{3,2},{4,0},{5,1},{6,7},{7,6},{8,12},{9,13},{10,... | collective-permute-start | bytes 4718600 | tf_op jit(solution)/shard_map/ppermute | solution.py:344
  510.7 31.1 %collective-permute-start.54 = (bf16[256,2560]{1,0:T(8,128)(2,1)}, bf16[256,2560]{1,0:T(8,128)(2,1)}, u32[]{:S(2)}, u32[]{:S(2)}) collective-permute-start(bf16[256,2560]{1,0:T(8,128)(2,1)} %fusion.6), channel_id=1, source_target_pairs={{0,1},{1,0},{2,6},{3,7},{4,5},{5,4},{6,2},{7,3},{8,9},{9,8},{10,14... | collective-permute-start | bytes 3932168 | tf_op jit(solution)/shard_map/ppermute | solution.py:346
  525.8 35.6 %collective-permute-start.20 = (bf16[2,256,1536]{2,1,0:T(8,128)(2,1)S(1)}, bf16[2,256,1536]{2,1,0:T(8,128)(2,1)S(1)}, u32[]{:S(2)}, u32[]{:S(2)}) collective-permute-start(bf16[2,256,1536]{2,1,0:T(8,128)(2,1)S(1)} %get-tuple-element.55), channel_id=1, source_target_pairs={{0,4},{1,5},{2,3},{3,2},{4,0},{5,1},{6,7},{7,6},{8,12},{9,13},{10,... | collective-permute-start | bytes 4718600 | tf_op jit(solution)/shard_map/ppermute | solution.py:344
  531.5 42.1 %collective-permute-start.50 = (bf16[256,2048]{1,0:T(8,128)(2,1)S(1)}, bf16[256,2048]{1,0:T(8,128)(2,1)S(1)}, u32[]{:S(2)}, u32[]{:S(2)}) collective-permute-start(bf16[256,2048]{1,0:T(8,128)(2,1)S(1)} %fusion.1), channel_id=1, source_target_pairs={{0,8},{24,16},{1,9},{25,17},{2,10},{26,18},{3,11},{27,19},{4,12},{... | collective-permute-start | bytes 3145736 | tf_op jit(solution)/shard_map/ppermute | solution.py:352
  541.8 33.2 %collective-permute-start.28 = (bf16[256,1536]{1,0:T(8,128)(2,1)S(1)}, bf16[256,1536]{1,0:T(8,128)(2,1)S(1)}, u32[]{:S(2)}, u32[]{:S(2)}) collective-permute-start(bf16[256,1536]{1,0:T(8,128)(2,1)S(1)} %fusion.9), channel_id=1, source_target_pairs={{0,1},{1,0},{2,6},{3,7},{4,5},{5,4},{6,2},{7,3},{8,9},{9,8},{10,14... | collective-permute-start | bytes 2359304 | tf_op jit(solution)/shard_map/ppermute | solution.py:346
  561.4 30.7 %collective-permute-start.55 = (bf16[256,2560]{1,0:T(8,128)(2,1)S(1)}, bf16[256,2560]{1,0:T(8,128)(2,1)S(1)}, u32[]{:S(2)}, u32[]{:S(2)}) collective-permute-start(bf16[256,2560]{1,0:T(8,128)(2,1)S(1)} %fusion), channel_id=1, source_target_pairs={{0,8},{24,16},{1,9},{25,17},{2,10},{26,18},{3,11},{27,19},{4,12},{... | collective-permute-start | bytes 3932168 | tf_op jit(solution)/shard_map/ppermute | solution.py:352
  571.7 21.5 %collective-permute-start.62 = (bf16[256,512]{1,0:T(8,128)(2,1)S(1)}, bf16[256,512]{1,0:T(8,128)(2,1)S(1)}, u32[]{:S(2)}, u32[]{:S(2)}) collective-permute-start(bf16[256,512]{1,0:T(8,128)(2,1)S(1)} %slice.129), channel_id=1, source_target_pairs={{0,0},{1,4},{2,2},{3,6},{4,1},{5,5},{6,3},{7,7},{8,8},{9,12},{10,1... | collective-permute-start | bytes 786440 | tf_op jit(solution)/shard_map/ppermute | solution.py:356
  573.6 31.4 %collective-permute-start.47 = (bf16[256,1536]{1,0:T(8,128)(2,1)}, bf16[256,1536]{1,0:T(8,128)(2,1)S(1)}, u32[]{:S(2)}, u32[]{:S(2)}) collective-permute-start(bf16[256,1536]{1,0:T(8,128)(2,1)} %collective-permute-done.46), channel_id=1, source_target_pairs={{8,0},{16,24},{9,1},{17,25},{10,2},{18,26},{11,3},{19,27},{12,4},{... | collective-permute-start | bytes 2359304 | tf_op jit(solution)/shard_map/ppermute | solution.py:352
  575.0 27.3 %collective-permute-start.51 = (bf16[256,2048]{1,0:T(8,128)(2,1)S(1)}, bf16[256,2048]{1,0:T(8,128)(2,1)S(1)}, u32[]{:S(2)}, u32[]{:S(2)}) collective-permute-start(bf16[256,2048]{1,0:T(8,128)(2,1)S(1)} %collective-permute-done.50), channel_id=1, source_target_pairs={{8,16},{16,8},{9,17},{17,9},{10,18},{18,10},{11,19},{19,11},{12,20... | collective-permute-start | bytes 3145736 | tf_op jit(solution)/shard_map/ppermute | solution.py:352
  578.0 31.9 %collective-permute-start.29 = (bf16[256,1536]{1,0:T(8,128)(2,1)S(1)}, bf16[256,1536]{1,0:T(8,128)(2,1)S(1)}, u32[]{:S(2)}, u32[]{:S(2)}) collective-permute-start(bf16[256,1536]{1,0:T(8,128)(2,1)S(1)} %fusion.4), channel_id=1, source_target_pairs={{0,8},{24,16},{1,9},{25,17},{2,10},{26,18},{3,11},{27,19},{4,12},{... | collective-permute-start | bytes 2359304 | tf_op jit(solution)/shard_map/ppermute | solution.py:352
  592.1 11.5 %collective-permute-start.56 = (bf16[256,2560]{1,0:T(8,128)(2,1)S(1)}, bf16[256,2560]{1,0:T(8,128)(2,1)S(1)}, u32[]{:S(2)}, u32[]{:S(2)}) collective-permute-start(bf16[256,2560]{1,0:T(8,128)(2,1)S(1)} %collective-permute-done.55), channel_id=1, source_target_pairs={{8,16},{16,8},{9,17},{17,9},{10,18},{18,10},{11,19},{19,11},{12,20... | collective-permute-start | bytes 3932168 | tf_op jit(solution)/shard_map/ppermute | solution.py:352
  593.2 32.6 %collective-permute-start.22 = (bf16[256,1536]{1,0:T(8,128)(2,1)S(1)}, bf16[256,1536]{1,0:T(8,128)(2,1)S(1)}, u32[]{:S(2)}, u32[]{:S(2)}) collective-permute-start(bf16[256,1536]{1,0:T(8,128)(2,1)S(1)} %fusion.5), channel_id=1, source_target_pairs={{0,8},{24,16},{1,9},{25,17},{2,10},{26,18},{3,11},{27,19},{4,12},{... | collective-permute-start | bytes 2359304 | tf_op jit(solution)/shard_map/ppermute | solution.py:352
  602.3 27.3 %collective-permute-start.52 = (bf16[256,2048]{1,0:T(8,128)(2,1)S(1)}, bf16[256,2048]{1,0:T(8,128)(2,1)S(1)}, u32[]{:S(2)}, u32[]{:S(2)}) collective-permute-start(bf16[256,2048]{1,0:T(8,128)(2,1)S(1)} %collective-permute-done.51), channel_id=1, source_target_pairs={{8,0},{16,24},{9,1},{17,25},{10,2},{18,26},{11,3},{19,27},{12,4},{... | collective-permute-start | bytes 3145736 | tf_op jit(solution)/shard_map/ppermute | solution.py:352
  603.6 54.6 %collective-permute-start.57 = (bf16[256,2560]{1,0:T(8,128)(2,1)S(1)}, bf16[256,2560]{1,0:T(8,128)(2,1)S(1)}, u32[]{:S(2)}, u32[]{:S(2)}) collective-permute-start(bf16[256,2560]{1,0:T(8,128)(2,1)S(1)} %collective-permute-done.56), channel_id=1, source_target_pairs={{8,0},{16,24},{9,1},{17,25},{10,2},{18,26},{11,3},{19,27},{12,4},{... | collective-permute-start | bytes 3932168 | tf_op jit(solution)/shard_map/ppermute | solution.py:352
  605.1 32.1 %collective-permute-start.58 = (bf16[256,1536]{1,0:T(8,128)(2,1)S(1)}, bf16[256,1536]{1,0:T(8,128)(2,1)S(1)}, u32[]{:S(2)}, u32[]{:S(2)}) collective-permute-start(bf16[256,1536]{1,0:T(8,128)(2,1)S(1)} %get-tuple-element.76), channel_id=1, source_target_pairs={{2,0},{6,4},{3,1},{7,5},{10,8},{14,12},{11,9},{15,13},{18,16},{22,... | collective-permute-start | bytes 2359304 | tf_op jit(solution)/shard_map/ppermute | solution.py:358
  609.9 30.3 %collective-permute-start.30 = (bf16[256,1536]{1,0:T(8,128)(2,1)S(1)}, bf16[256,1536]{1,0:T(8,128)(2,1)S(1)}, u32[]{:S(2)}, u32[]{:S(2)}) collective-permute-start(bf16[256,1536]{1,0:T(8,128)(2,1)S(1)} %collective-permute-done.29), channel_id=1, source_target_pairs={{8,16},{16,8},{9,17},{17,9},{10,18},{18,10},{11,19},{19,11},{12,20... | collective-permute-start | bytes 2359304 | tf_op jit(solution)/shard_map/ppermute | solution.py:352
  625.8 17.6 %collective-permute-start.23 = (bf16[256,1536]{1,0:T(8,128)(2,1)S(1)}, bf16[256,1536]{1,0:T(8,128)(2,1)S(1)}, u32[]{:S(2)}, u32[]{:S(2)}) collective-permute-start(bf16[256,1536]{1,0:T(8,128)(2,1)S(1)} %collective-permute-done.22), channel_id=1, source_target_pairs={{8,16},{16,8},{9,17},{17,9},{10,18},{18,10},{11,19},{19,11},{12,20... | collective-permute-start | bytes 2359304 | tf_op jit(solution)/shard_map/ppermute | solution.py:352
  635.2 30.3 %collective-permute-start.59 = (bf16[256,1536]{1,0:T(8,128)(2,1)S(1)}, bf16[256,1536]{1,0:T(8,128)(2,1)S(1)}, u32[]{:S(2)}, u32[]{:S(2)}) collective-permute-start(bf16[256,1536]{1,0:T(8,128)(2,1)S(1)} %get-tuple-element.74), channel_id=1, source_target_pairs={{2,0},{6,4},{3,1},{7,5},{10,8},{14,12},{11,9},{15,13},{18,16},{22,... | collective-permute-start | bytes 2359304 | tf_op jit(solution)/shard_map/ppermute | solution.py:358
  637.2 24.6 %collective-permute-start.63 = (bf16[256,1024]{1,0:T(8,128)(2,1)S(1)}, bf16[256,1024]{1,0:T(8,128)(2,1)S(1)}, u32[]{:S(2)}, u32[]{:S(2)}) collective-permute-start(bf16[256,1024]{1,0:T(8,128)(2,1)S(1)} %slice.130), channel_id=1, source_target_pairs={{0,0},{1,4},{2,2},{3,6},{4,1},{5,5},{6,3},{7,7},{8,8},{9,12},{10,1... | collective-permute-start | bytes 1572872 | tf_op jit(solution)/shard_map/ppermute | solution.py:356
  640.2 75.7 %collective-permute-start.64 = (bf16[256,1536]{1,0:T(8,128)(2,1)S(1)}, bf16[256,1536]{1,0:T(8,128)(2,1)S(1)}, u32[]{:S(2)}, u32[]{:S(2)}) collective-permute-start(bf16[256,1536]{1,0:T(8,128)(2,1)S(1)} %slice.131), channel_id=1, source_target_pairs={{0,0},{1,4},{2,2},{3,6},{4,1},{5,5},{6,3},{7,7},{8,8},{9,12},{10,1... | collective-permute-start | bytes 2359304 | tf_op jit(solution)/shard_map/ppermute | solution.py:356
  643.4 76.9 %collective-permute-start.31 = (bf16[256,1536]{1,0:T(8,128)(2,1)S(1)}, bf16[256,1536]{1,0:T(8,128)(2,1)S(1)}, u32[]{:S(2)}, u32[]{:S(2)}) collective-permute-start(bf16[256,1536]{1,0:T(8,128)(2,1)S(1)} %collective-permute-done.30), channel_id=1, source_target_pairs={{8,0},{16,24},{9,1},{17,25},{10,2},{18,26},{11,3},{19,27},{12,4},{... | collective-permute-start | bytes 2359304 | tf_op jit(solution)/shard_map/ppermute | solution.py:352
  658.1 53.2 %collective-permute-start.24 = (bf16[256,1536]{1,0:T(8,128)(2,1)S(1)}, bf16[256,1536]{1,0:T(8,128)(2,1)S(1)}, u32[]{:S(2)}, u32[]{:S(2)}) collective-permute-start(bf16[256,1536]{1,0:T(8,128)(2,1)S(1)} %collective-permute-done.23), channel_id=1, source_target_pairs={{8,0},{16,24},{9,1},{17,25},{10,2},{18,26},{11,3},{19,27},{12,4},{... | collective-permute-start | bytes 2359304 | tf_op jit(solution)/shard_map/ppermute | solution.py:352
  661.8 55.2 %collective-permute-start.67 = (bf16[256,1024]{1,0:T(8,128)(2,1)S(1)}, bf16[256,1024]{1,0:T(8,128)(2,1)S(1)}, u32[]{:S(2)}, u32[]{:S(2)}) collective-permute-start(bf16[256,1024]{1,0:T(8,128)(2,1)S(1)} %collective-permute-done.63.refs_9_), channel_id=1, source_target_pairs={{0,2},{2,0},{4,6},{6,4},{1,3},{3,1},{5,7},{7,5},{8,10},{10,8},{12,... | collective-permute-start | bytes 1572872 | tf_op jit(solution)/shard_map/ppermute | solution.py:359
  665.5 57.9 %collective-permute-start.60 = (bf16[256,2048]{1,0:T(8,128)(2,1)S(1)}, bf16[256,2048]{1,0:T(8,128)(2,1)S(1)}, u32[]{:S(2)}, u32[]{:S(2)}) collective-permute-start(bf16[256,2048]{1,0:T(8,128)(2,1)S(1)} %get-tuple-element.72), channel_id=1, source_target_pairs={{0,2},{4,6},{1,3},{5,7},{8,10},{12,14},{9,11},{13,15},{16,18},{20,... | collective-permute-start | bytes 3145736 | tf_op jit(solution)/shard_map/ppermute | solution.py:358
  711.3 26.7 %collective-permute-start.65 = (bf16[256,2048]{1,0:T(8,128)(2,1)S(1)}, bf16[256,2048]{1,0:T(8,128)(2,1)S(1)}, u32[]{:S(2)}, u32[]{:S(2)}) collective-permute-start(bf16[256,2048]{1,0:T(8,128)(2,1)S(1)} %slice.132), channel_id=1, source_target_pairs={{0,0},{1,4},{2,2},{3,6},{4,1},{5,5},{6,3},{7,7},{8,8},{9,12},{10,1... | collective-permute-start | bytes 3145736 | tf_op jit(solution)/shard_map/ppermute | solution.py:356
  716.0 25.0 %collective-permute-start.68 = (bf16[256,1536]{1,0:T(8,128)(2,1)S(1)}, bf16[256,1536]{1,0:T(8,128)(2,1)S(1)}, u32[]{:S(2)}, u32[]{:S(2)}) collective-permute-start(bf16[256,1536]{1,0:T(8,128)(2,1)S(1)} %collective-permute-done.64.refs_10_), channel_id=1, source_target_pairs={{0,2},{2,0},{4,6},{6,4},{1,3},{3,1},{5,7},{7,5},{8,10},{10,8},{12,... | collective-permute-start | bytes 2359304 | tf_op jit(solution)/shard_map/ppermute | solution.py:359
  717.0 50.4 %collective-permute-start.34 = (bf16[256,1536]{1,0:T(8,128)(2,1)S(1)}, bf16[256,1536]{1,0:T(8,128)(2,1)S(1)}, u32[]{:S(2)}, u32[]{:S(2)}) collective-permute-start(bf16[256,1536]{1,0:T(8,128)(2,1)S(1)} %get-tuple-element.80), channel_id=1, source_target_pairs={{0,0},{1,4},{2,2},{3,6},{4,1},{5,5},{6,3},{7,7},{8,8},{9,12},{10,1... | collective-permute-start | bytes 2359304 | tf_op jit(solution)/shard_map/ppermute | solution.py:356
  720.3 48.9 %collective-permute-start.61 = (bf16[256,2560]{1,0:T(8,128)(2,1)S(1)}, bf16[256,2560]{1,0:T(8,128)(2,1)S(1)}, u32[]{:S(2)}, u32[]{:S(2)}) collective-permute-start(bf16[256,2560]{1,0:T(8,128)(2,1)S(1)} %get-tuple-element.70), channel_id=1, source_target_pairs={{0,2},{4,6},{1,3},{5,7},{8,10},{12,14},{9,11},{13,15},{16,18},{20,... | collective-permute-start | bytes 3932168 | tf_op jit(solution)/shard_map/ppermute | solution.py:358
  723.4 42.7 %collective-permute-start.35 = (bf16[256,1024]{1,0:T(8,128)(2,1)S(1)}, bf16[256,1024]{1,0:T(8,128)(2,1)S(1)}, u32[]{:S(2)}, u32[]{:S(2)}) collective-permute-start(bf16[256,1024]{1,0:T(8,128)(2,1)S(1)} %slice.120), channel_id=1, source_target_pairs={{0,0},{1,4},{2,2},{3,6},{4,1},{5,5},{6,3},{7,7},{8,8},{9,12},{10,1... | collective-permute-start | bytes 1572872 | tf_op jit(solution)/shard_map/ppermute | solution.py:356
  738.1 31.3 %collective-permute-start.69 = (bf16[256,2048]{1,0:T(8,128)(2,1)S(1)}, bf16[256,2048]{1,0:T(8,128)(2,1)S(1)}, u32[]{:S(2)}, u32[]{:S(2)}) collective-permute-start(bf16[256,2048]{1,0:T(8,128)(2,1)S(1)} %collective-permute-done.65.refs_11_), channel_id=1, source_target_pairs={{0,2},{2,0},{4,6},{6,4},{1,3},{3,1},{5,7},{7,5},{8,10},{10,8},{12,... | collective-permute-start | bytes 3145736 | tf_op jit(solution)/shard_map/ppermute | solution.py:359
  740.9 52.1 %collective-permute-start.33 = (bf16[256,1536]{1,0:T(8,128)(2,1)S(1)}, bf16[256,1536]{1,0:T(8,128)(2,1)S(1)}, u32[]{:S(2)}, u32[]{:S(2)}) collective-permute-start(bf16[256,1536]{1,0:T(8,128)(2,1)S(1)} %get-tuple-element.78), channel_id=1, source_target_pairs={{0,2},{4,6},{1,3},{5,7},{8,10},{12,14},{9,11},{13,15},{16,18},{20,... | collective-permute-start | bytes 2359304 | tf_op jit(solution)/shard_map/ppermute | solution.py:358
  766.2 26.9 %collective-permute-start.32 = (bf16[256,1536]{1,0:T(8,128)(2,1)S(1)}, bf16[256,1536]{1,0:T(8,128)(2,1)S(1)}, u32[]{:S(2)}, u32[]{:S(2)}) collective-permute-start(bf16[256,1536]{1,0:T(8,128)(2,1)S(1)} %get-tuple-element.80), channel_id=1, source_target_pairs={{0,2},{4,6},{1,3},{5,7},{8,10},{12,14},{9,11},{13,15},{16,18},{20,... | collective-permute-start | bytes 2359304 | tf_op jit(solution)/shard_map/ppermute | solution.py:358
  767.5 25.6 %collective-permute-start.36 = (bf16[256,1536]{1,0:T(8,128)(2,1)S(1)}, bf16[256,1536]{1,0:T(8,128)(2,1)S(1)}, u32[]{:S(2)}, u32[]{:S(2)}) collective-permute-start(bf16[256,1536]{1,0:T(8,128)(2,1)S(1)} %collective-permute-done.34.refs_4_), channel_id=1, source_target_pairs={{0,2},{2,0},{4,6},{6,4},{1,3},{3,1},{5,7},{7,5},{8,10},{10,8},{12,... | collective-permute-start | bytes 2359304 | tf_op jit(solution)/shard_map/ppermute | solution.py:359
  769.2 23.9 %collective-permute-start.37 = (bf16[256,1024]{1,0:T(8,128)(2,1)S(1)}, bf16[256,1024]{1,0:T(8,128)(2,1)S(1)}, u32[]{:S(2)}, u32[]{:S(2)}) collective-permute-start(bf16[256,1024]{1,0:T(8,128)(2,1)S(1)} %collective-permute-done.35.refs_5_), channel_id=1, source_target_pairs={{0,2},{2,0},{4,6},{6,4},{1,3},{3,1},{5,7},{7,5},{8,10},{10,8},{12,... | collective-permute-start | bytes 1572872 | tf_op jit(solution)/shard_map/ppermute | solution.py:359
  (29 other events, 565.3 us)
